TPU v7x, 128 devices: a whole 4x4x4 slice. The times are simulated.
128 devices in a mesh: ctx: 16 (over z, y_lo, core), tp: 8 (over y_hi, x).
Axes of the slice: x: 4, y: 4 (y_hi: 2, y_lo: 2; y = y_hi * 2 + y_lo), z: 4, core: 2. Of those that a mesh axis runs over, the one named last changes fastest.
Arguments:
- inner_x: bfloat16 [2, 2048, 16384], P(None, 'ctx', 'tp'), may hold values from -6 to 6
- gate_z: bfloat16 [2, 2048, 16384], P(None, 'ctx', 'tp'), may hold values from -6 to 6
- proj_bc: bfloat16 [2, 2048, 8, 512], P(None, 'ctx', 'tp'), may hold values from -6 to 6
- dt_raw: float32 [2, 256, 2048], P(None, 'tp', 'ctx'), may hold values from -6 to 82
- a_log: float32 [256], P('tp'), may hold values from -10 to 1
- dt_bias: float32 [256], P('tp'), may hold values from -0.5 to 0.5
- d_skip: float32 [256], P('tp'), may hold values from 0.5 to 1.5
- conv_x: float32 [4, 16384], P(None, 'tp'), may hold values from -3 to 3
- conv_bc: float32 [4, 8, 512], P(None, 'tp'), may hold values from -3 to 3
- bias_x: float32 [16384], P('tp'), may hold values from -0.5 to 0.5
- bias_bc: float32 [8, 512], P('tp'), may hold values from -0.5 to 0.5
- norm_gain: float32 [16384], P('tp'), may hold values from 0.25 to 1.75
- init_state: float32 [2, 256, 64, 256], P(None, 'tp'), may hold values from -6 to 6
- init_conv_x: bfloat16 [2, 3, 16384], P(None, None, 'tp'), may hold values from -6 to 6
- init_conv_bc: bfloat16 [2, 3, 8, 512], P(None, None, 'tp'), may hold values from -6 to 6
- lengths: int32 [2], replicated, may hold values from 1024 to 2048, as said below
- dec_x: bfloat16 [4, 128, 16384], P(None, 'ctx', 'tp'), may hold values from -6 to 6
- dec_z: bfloat16 [4, 128, 16384], P(None, 'ctx', 'tp'), may hold values from -6 to 6
- dec_bc: bfloat16 [4, 128, 8, 512], P(None, 'ctx', 'tp'), may hold values from -6 to 6
- dec_dt: float32 [4, 256, 128], P(None, 'tp', 'ctx'), may hold values from -2.5 to 1
- row_prompt: int32 [128], P('ctx'), may hold values from 0 to 1
- w_out: bfloat16 [16384, 8192], P('tp', 'ctx'), may hold values from -0.046875 to 0.046875
Outputs:
- prefill_out: bfloat16 [2, 2048, 16384], P(None, 'ctx', 'tp')
- layer_out: bfloat16 [4, 128, 8192], P(None, 'tp', 'ctx')
Inputs may be any that keep to these rules, and one draw needn't show every extreme that they name: Positions from lengths[s] on are padding of prompt s. At least one prompt has all 2048 positions live.
All inputs are finite; a program needn't handle non-finite values.
Results may differ from a plain program's by a relative error of at most 0.005.
Values may be sent and summed in bfloat16 or wider, within the bound.
A program may use at most 256 MiB of HBM per device.

v0:
```python
import jax
import jax.numpy as jnp
from jax import lax
from jax.sharding import Mesh
from jax.sharding import PartitionSpec as P

HEADS = 256
HEAD_DIM = 64
GROUPS = 8
CTX = ("ctx_0", "ctx_1", "ctx_2")


epsilon = 1e-05
highest = lax.Precision.HIGHEST


def from_behind(value, axis, by):
    peers = lax.axis_size(axis)
    pairs = [(i, i + by) for i in range(peers) if 0 <= i + by < peers]
    return lax.ppermute(value, axis, pairs)


def nothing_yet(value, identity):
    return jax.tree.map(
        lambda a, e: jnp.broadcast_to(jnp.asarray(e, a.dtype), a.shape), value, identity
    )


def carried_in(value, axes, combine, identity):
    before = start = nothing_yet(value, identity)
    subtotal = value
    for axis in reversed(axes):
        peers, place = (lax.axis_size(axis), lax.axis_index(axis))
        pieces = jax.tree.map(lambda part: lax.all_gather(part, axis), subtotal)
        inside, subtotal = (start, start)
        for k in range(peers):
            passed = k < place
            subtotal = combine(subtotal, jax.tree.map(lambda part: part[k], pieces))
            inside = jax.tree.map(lambda new, old: jnp.where(passed, new, old), subtotal, inside)
        before = combine(inside, before)
    return before


def from_everyone(value, axis):
    copies = jnp.broadcast_to(value, (lax.axis_size(axis), *value.shape))
    return lax.all_to_all(copies, axis, split_axis=0, concat_axis=0, tiled=True)


def combined_pairwise(pieces, combine):
    while len(jax.tree.leaves(pieces)[0]) > 1:
        pieces = jax.vmap(combine)(*(pieces[side::2] for side in (0, 1)))
    return pieces[0]


def prefix(value, axis, combine, identity):
    peers, place = (lax.axis_size(axis), lax.axis_index(axis))
    passed = jnp.arange(peers) > place

    def kept(part, zero, own):
        part = jnp.where(
            passed.reshape(-1, *(1 for _ in own.shape)), part, jnp.asarray(zero, own.dtype)
        )
        return part[::-1]

    pieces = from_everyone(value, axis)
    return combined_pairwise(kept(pieces, identity, value), combine)


def in_one(arrays, axis):
    ends = [0]
    for a in arrays:
        ends.append(ends[-1] + a.size)
    subtotal = lax.psum(jnp.concatenate([a.ravel() for a in arrays]), axis)
    return tuple((subtotal[b:e].reshape(a.shape) for a, b, e in zip(arrays, ends, ends[1:])))


def split_up(value, dim, peers):
    shape = value.shape
    blocks = value.reshape(*shape[:dim], peers, shape[dim] // peers, *shape[dim + 1 :])
    return jnp.moveaxis(blocks, dim, 0)


def summed_on_arrival(value, axis, dim):
    peers = lax.axis_size(axis)
    blocks = lax.all_to_all(split_up(value, dim, peers), axis, 0, 0, tiled=True)
    return jnp.sum(blocks, axis=0)


def gated_norm(values, gate, gain, group_width):
    mixed = values * jax.nn.silu(gate)
    shape = mixed.shape
    grouped = mixed.reshape(shape[:-1] + (shape[-1] // group_width, group_width))
    scaled = grouped * lax.rsqrt(jnp.mean(grouped * grouped, axis=-1, keepdims=True) + epsilon)
    return scaled.reshape(shape) * gain


def chain(earlier, later):
    return (earlier[0] * later[0], later[0][..., None, None] * earlier[1] + later[1])


def product(earlier, later):
    return earlier * later


def local_mixing(items):
    c_one, b_one, running_one, step_one, values_one = items
    tokens = c_one.shape[0]
    scores = jnp.einsum("tgn,ugn->gtu", c_one, b_one, precision=highest)
    lower = jnp.arange(tokens)[:, None] >= jnp.arange(tokens)[None, :]
    gap = running_one[..., :, None] - running_one[..., None, :]
    mixing = (
        jnp.where(lower, jnp.exp(jnp.where(lower, gap, 0.0)), 0.0)
        * scores[:, None]
        * step_one[..., None, :]
    )
    return jnp.einsum("ghtu,ughp->tghp", mixing, values_one, precision=highest)


def shards(
    inner_x,
    gate_z,
    proj_bc,
    dt_raw,
    a_log,
    dt_bias,
    d_skip,
    conv_x,
    conv_bc,
    bias_x,
    bias_bc,
    norm_gain,
    init_state,
    init_conv_x,
    init_conv_bc,
    lengths,
    dec_x,
    dec_z,
    dec_bc,
    dec_dt,
    row_prompt,
    w_out,
):
    prompts, tokens, width = inner_x.shape
    groups_here, pair_width = (proj_bc.shape[2], proj_bc.shape[3])
    state_size = pair_width // 2
    heads_here = dt_raw.shape[1]
    per_group = heads_here // groups_here
    head_size = width // heads_here
    taps = conv_x.shape[0]
    group_width = HEADS * HEAD_DIM // GROUPS
    device = lax.axis_index(CTX)
    flat_bc = proj_bc.reshape(prompts, tokens, groups_here * pair_width)
    raw = jnp.concatenate([inner_x, flat_bc], axis=-1)
    rim = from_behind(raw[:, tokens - taps + 1 :], CTX, 1)
    start_rim = jnp.concatenate([init_conv_x, init_conv_bc.reshape(prompts, taps - 1, -1)], axis=-1)
    rim = jnp.where(device == 0, start_rim, rim)
    padded = jnp.concatenate([rim, raw], axis=1).astype(jnp.float32)
    tap_weights = jnp.concatenate([conv_x, conv_bc.reshape(taps, -1)], axis=-1)
    tap_bias = jnp.concatenate([bias_x, bias_bc.reshape(-1)], axis=-1)
    total = tap_bias
    for offset in range(taps):
        total = total + tap_weights[offset] * padded[:, offset : offset + tokens]
    active = jax.nn.silu(total)
    values = active[..., :width].reshape(prompts, tokens, groups_here, per_group, head_size)
    mixers = active[..., width:].reshape(prompts, tokens, groups_here, pair_width)
    b_part = mixers[..., :state_size]
    c_part = mixers[..., state_size:]
    places = device * tokens + jnp.arange(tokens, dtype=jnp.int32)
    live = (places[None, :] < lengths[:, None]).astype(jnp.float32)
    rate = jnp.exp(a_log)
    step_size = jax.nn.softplus(dt_raw + dt_bias[None, :, None]) * live[:, None, :]
    log_decay = -rate[None, :, None] * step_size
    running = jnp.cumsum(log_decay, axis=2).reshape(prompts, groups_here, per_group, tokens)
    step_group = step_size.reshape(prompts, groups_here, per_group, tokens)
    y_local = lax.map(local_mixing, (c_part, b_part, running, step_group, values))
    span_decay = jnp.exp(running[..., -1])
    to_end = jnp.exp(running[..., -1:] - running) * step_group
    weighted = values * jnp.transpose(to_end, (0, 3, 1, 2))[..., None]
    own_state = jnp.einsum("sughp,sugn->sghpn", weighted, b_part, precision=highest)
    start_state = init_state.reshape(prompts, groups_here, per_group, head_size, state_size)
    prefix_decay, prefix_state = carried_in(
        (span_decay, own_state), CTX, chain, (jnp.ones_like(span_decay), jnp.zeros_like(own_state))
    )
    entry_state = prefix_decay[..., None, None] * start_state + prefix_state
    y_carried = (
        jnp.einsum("stgn,sghpn->stghp", c_part, entry_state, precision=highest)
        * jnp.exp(jnp.transpose(running, (0, 3, 1, 2)))[..., None]
    )
    mixed_y = y_local + y_carried + d_skip.reshape(groups_here, per_group)[:, :, None] * values
    prefill_out = gated_norm(
        mixed_y.reshape(prompts, tokens, width), gate_z.astype(jnp.float32), norm_gain, group_width
    ).astype(jnp.bfloat16)
    target = lengths[:, None] - (taps - 1) + jnp.arange(taps - 1, dtype=jnp.int32)[None, :]
    picker = (places[None, None, :] == target[:, :, None]).astype(jnp.bfloat16)
    tail_terms = jnp.einsum("sjt,stc->sjc", picker, raw, preferred_element_type=jnp.float32)
    suffix = prefix(span_decay, CTX, product, jnp.ones_like(span_decay))
    first_term = jnp.where(device == 0, 1.0, 0.0) * span_decay[..., None, None] * start_state
    final, tails = in_one((suffix[..., None, None] * (own_state + first_term), tail_terms), CTX)
    steps = dec_x.shape[0]
    batch = dec_x.shape[1]
    pick = (row_prompt[:, None] == jnp.arange(prompts, dtype=jnp.int32)[None, :]).astype(
        jnp.float32
    )
    state = jnp.einsum("rs,sghpn->rghpn", pick, final, precision=highest)
    window = jnp.einsum("rs,sjc->rjc", pick, tails, precision=highest)
    fresh_all = jnp.concatenate([dec_x, dec_bc.reshape(steps, batch, -1)], axis=-1)
    rate_group = rate.reshape(groups_here, per_group)
    skip_group = d_skip.reshape(groups_here, per_group)
    hidden = []
    for moment in range(steps):
        full = jnp.concatenate([window, fresh_all[moment][:, None].astype(jnp.float32)], axis=1)
        total = tap_bias
        for offset in range(taps):
            total = total + tap_weights[offset] * full[:, offset]
        active = jax.nn.silu(total)
        row_values = active[:, :width].reshape(batch, groups_here, per_group, head_size)
        row_mixers = active[:, width:].reshape(batch, groups_here, pair_width)
        step_row = jax.nn.softplus(dec_dt[moment] + dt_bias[:, None]).T.reshape(
            batch, groups_here, per_group
        )
        keep = jnp.exp(-rate_group * step_row)
        state = (
            keep[..., None, None] * state
            + (step_row[..., None] * row_values)[..., None]
            * row_mixers[:, :, None, None, :state_size]
        )
        y_row = (
            jnp.einsum("rghpn,rgn->rghp", state, row_mixers[..., state_size:], precision=highest)
            + skip_group[:, :, None] * row_values
        )
        hidden.append(
            gated_norm(
                y_row.reshape(batch, width),
                dec_z[moment].astype(jnp.float32),
                norm_gain,
                group_width,
            ).astype(jnp.bfloat16)
        )
        window = full[:, 1:]
    dec_hidden = jnp.stack(hidden)
    flat = jnp.dot(
        lax.all_gather(dec_hidden, CTX, axis=1, tiled=True).reshape(-1, width),
        w_out,
        preferred_element_type=jnp.float32,
    )
    terms = flat.reshape(steps, -1, w_out.shape[1])
    layer_out = summed_on_arrival(terms, "tp", 1).astype(jnp.bfloat16)
    return (prefill_out, layer_out)


def solution(mesh):
    split = Mesh(mesh.devices.reshape(4, 2, 2, mesh.shape["tp"]), ("ctx_0", "ctx_1", "ctx_2", "tp"))
    placed = (
        P(None, CTX, "tp"),
        P(None, CTX, "tp"),
        P(None, CTX, "tp", None),
        P(None, "tp", CTX),
        P("tp"),
        P("tp"),
        P("tp"),
        P(None, "tp"),
        P(None, "tp", None),
        P("tp"),
        P("tp", None),
        P("tp"),
        P(None, "tp", None, None),
        P(None, None, "tp"),
        P(None, None, "tp", None),
        P(),
        P(None, CTX, "tp"),
        P(None, CTX, "tp"),
        P(None, CTX, "tp", None),
        P(None, "tp", CTX),
        P(CTX),
        P("tp", CTX),
    )
    return jax.shard_map(
        shards,
        mesh=split,
        in_specs=placed,
        out_specs=(P(None, CTX, "tp"), P(None, "tp", CTX)),
        check_vma=False,
    )
```

profile of v0, /device:TPU:1, one launch (start us, length us, event | category | flops | bytes accessed | tf_op | source)
XLA Modules:
  0.0 611.3 jit_solution(18311368677836457388)
XLA Ops:
  9.7 4.6 collective-permute-start
  19.3 6.2 %all-to-all-start = ((f32[16,2,1,32]{3,1,2,0:T(2,128)}), f32[16,2,1,32]{3,1,2,0:T(2,128)}, u32[]{:S(2)}, u32[]{:S(2)}) async-start(f32[16,2,1,32]{3,1,2,0:T(2,128)} %broadcast_in_dim.46), calls=%async_computation | async-start | bytes 32768 | tf_op jit(solution)/shard_map/all_to_all | solution.py:46
  47.5 8.9 %add_multiply_fusion = (f32[2,32,64,256]{3,2,1,0:T(8,128)S(1)}, f32[2,32,64,256]{3,2,1,0:T(8,128)}) fusion(f32[2,32,64,256]{3,2,1,0:T(8,128)} %param.36, f32[2,32]{1,0:T(2,128)S(1)} %get-tuple-element.126, f32[2,32]{1,0:T(2,128)S(1)} %copy-done.44, f32[2,128,1,512]{3,1,0,2:T(8,128)S(1)} %slice_bitcast_fusion.4, f32[2,128,32,64]{1,3,2,0:T(8,128)} %bitcast.361, ...), kind=kOutput, calls=%fused_computation.64 | convolution fusion | flops 1614282752 | bytes 14977024 | tf_op jit(solution)/shard_map/sughp,sugn->sghpn/dot_general | solution.py:179
  58.6 3.4 pad_maximum_fusion
  75.2 3.5 all-gather.2
  78.7 9.1 %all_gather.31 = f32[4,2,1,32]{3,1,2,0:T(2,128)S(1)} all-gather(f32[1,2,1,32]{3,1,2,0:T(2,128)S(1)} %bitcast.388), channel_id=1, replica_groups=mesh['ctx_0'=4,'ctx_1'=2,'ctx_2'=2,'tp'=8] {'ctx_0'}, dimensions={0}, use_global_device_ids=true | all-gather | bytes 1280 | tf_op jit(solution)/shard_map/all_gather | solution.py:34
  90.4 109.8 %all-reduce.2.cloned.1.call-done = f32[1063936]{0:T(1024)} async-done(((f32[1063936]{0:T(1024)}), f32[1063936]{0:T(1024)}) %all-reduce.2.cloned.1.call-update) | async-done | bytes 4255760 | tf_op jit(solution)/shard_map/psum | solution.py:73
  220.2 4.5 slice.384
  224.6 5.3 reshape.914
  236.2 3.2 broadcast_multiply_fusion.1
  239.4 6.1 fusion.51
  246.2 26.9 %multiply_add_fusion = (f32[8,32,64,256]{3,0,2,1:T(8,128)S(1)}, f32[8,32,64,256]{3,0,2,1:T(8,128)}, f32[8,32,64,256]{3,0,2,1:T(8,128)}, f32[8,32,64,256]{3,0,2,1:T(8,128)}) fusion(f32[8,256]{1,0:T(8,128)} %get-tuple-element.144, f32[8,32,64]{0,2,1:T(8,128)S(1)} %broadcast_multiply_fusion, f32[8,32]{0,1:T(8,128)S(1)} %copy-done.29, ...), kind=kOutput, calls=%fused_computation.36 | convolution fusion | flops 150994960 | bytes 71602208 | tf_op jit(solution)/shard_map/rs,sghpn->rghpn/dot_general | solution.py:204
  273.1 28.2 %fusion.35 = f32[8,1,32,64]{3,1,2,0:T(1,128)S(1)} fusion(f32[8,32,64,256]{3,0,2,1:T(8,128)} %get-tuple-element.167, f32[8,256,1,1]{1,0,2,3:T(8,128)S(1)} %copy-done.35), kind=kOutput, calls=%fused_computation.34 | convolution fusion | flops 50331648 | bytes 16850944 | tf_op jit(solution)/shard_map/rghpn,rgn->rghp/dot_general | solution.py:228
  301.3 28.3 %fusion.33 = f32[8,1,32,64]{3,1,2,0:T(1,128)S(1)} fusion(f32[8,32,64,256]{3,0,2,1:T(8,128)} %get-tuple-element.96, f32[8,256,1,1]{1,0,2,3:T(8,128)S(1)} %copy-done.33), kind=kOutput, calls=%fused_computation.32 | convolution fusion | flops 50331648 | bytes 16850944 | tf_op jit(solution)/shard_map/rghpn,rgn->rghp/dot_general | solution.py:228
  329.7 28.2 %fusion.31 = f32[8,1,32,64]{3,1,2,0:T(1,128)S(1)} fusion(f32[8,32,64,256]{3,0,2,1:T(8,128)} %get-tuple-element.95, f32[8,256,1,1]{1,0,2,3:T(8,128)S(1)} %copy-done.32), kind=kOutput, calls=%fused_computation.30 | convolution fusion | flops 50331648 | bytes 16850944 | tf_op jit(solution)/shard_map/rghpn,rgn->rghp/dot_general | solution.py:228
  358.0 22.4 %fusion.29 = f32[8,1,32,64]{3,1,2,0:T(1,128)S(1)} fusion(f32[8,32,64,256]{3,0,2,1:T(8,128)S(1)} %get-tuple-element.94, f32[8,256,1,1]{1,0,2,3:T(8,128)S(1)} %copy-done.34), kind=kOutput, calls=%fused_computation.28 | convolution fusion | flops 50331648 | bytes 16850944 | tf_op jit(solution)/shard_map/rghpn,rgn->rghp/dot_general | solution.py:228
  386.7 6.0 add_bitcast_fusion
  394.8 27.6 %all-gather.12.cloned.1.call-done = bf16[4,128,2048]{2,1,0:T(8,128)(2,1)} async-done(((bf16[4,8,2048]{2,1,0:T(8,128)(2,1)}), bf16[4,128,2048]{2,1,0:T(8,128)(2,1)}) %all-gather.12.cloned.1.call-update) | async-done | bytes 2097168 | tf_op jit(solution)/shard_map/all_gather | solution.py:242
  426.3 6.5 %all-to-all-start.1 = ((f32[8,4,16,512]{3,2,1,0:T(8,128)}), f32[8,4,16,512]{3,2,1,0:T(8,128)S(1)}, u32[]{:S(2)}, u32[]{:S(2)}) async-start(f32[8,4,16,512]{3,2,1,0:T(8,128)} %copy.143), calls=%async_computation.1 | async-start | bytes 2097152 | tf_op jit(solution)/shard_map/all_to_all | solution.py:85
  432.9 15.9 %while.10 = (s32[]{:T(128)}, f32[2,128,1,32,64]{1,4,3,2,0:T(8,128)}, f32[2,128,1,32,64]{1,4,3,2,0:T(8,128)}, f32[2,1,32,128]{3,2,1,0:T(8,128)S(1)}, f32[2,128,1,...) while((s32[]{:T(128)}, ...), condition=%wide.region_2.3_spmd, body=%wide.region_1.2_spmd.sunk | while | flops 455622656 | bytes 2639969 | solution.py:175
  434.1 6.7 %fusion.194 = f32[2,128,1,32,64]{1,4,3,2,0:T(8,128)} fusion(f32[2,128,1,32,64]{1,4,3,2,0:T(8,128)} %get-tuple-element.230, s32[]{:T(128)S(6)} %copy.198, f32[32,128]{1,0:T(8,128)S(1)} %get-tuple-element.219, f32[128,128]{1,0:T(8,128)S(1)} %fusion.193, f32[32,128]{1,0:T(8,128)S(1)} %get-tuple-element.220, ...), kind=kOutput, calls=%fused_computation.8.clone.1 | convolution fusion | flops 405274624 | bytes 2229248 | tf_op jit(solution)/shard_map/while/body/eval_jaxpr/ghtu,ughp->tghp/dot_general | solution.py:116
  442.1 6.7 %fusion.194 = f32[2,128,1,32,64]{1,4,3,2,0:T(8,128)} fusion(f32[2,128,1,32,64]{1,4,3,2,0:T(8,128)} %get-tuple-element.230, s32[]{:T(128)S(6)} %copy.198, f32[32,128]{1,0:T(8,128)S(1)} %get-tuple-element.219, f32[128,128]{1,0:T(8,128)S(1)} %fusion.193, f32[32,128]{1,0:T(8,128)S(1)} %get-tuple-element.220, ...), kind=kOutput, calls=%fused_computation.8.clone.1 | convolution fusion | flops 405274624 | bytes 2229248 | tf_op jit(solution)/shard_map/while/body/eval_jaxpr/ghtu,ughp->tghp/dot_general | solution.py:116
  450.9 126.6 %all-gather.10.cloned.1.call-done = f32[4,2,1,32,64,256]{5,4,3,2,1,0:T(8,128)} async-done(((f32[1,2,1,32,64,256]{5,4,3,2,1,0:T(8,128)}), f32[4,2,1,32,64,256]{5,4,3,2,1,0:T(8,128)}) %all-gather.10.cloned.1.call-update) | async-done | bytes 16777232 | tf_op jit(solution)/shard_map/all_gather | solution.py:34
  577.5 18.4 %fusion.86 = f32[2,128,1,32,64]{1,4,3,0,2:T(8,128)} fusion(f32[2,128,1,32,64]{1,4,3,2,0:T(8,128)} %get-tuple-element.39, f32[2,128,1,32,64]{1,4,3,0,2:T(8,128)} %bitcast.363, f32[4,2,1,32,64,256]{5,4,3,1,2,0:T(8,128)} %bitcast.390, f32[2,32,64,256]{3,2,1,0:T(8,128)} %param.36, f32[2,2,1,32,64,256]{5,4,3,1,2,0:T(8,128)} %bitcast.360, ...), kind=kOutput, calls=%fused_computation.103 | convolution fusion | flops 1641021440 | bytes 44339208 | tf_op jit(solution)/shard_map/stgn,sghpn->stghp/dot_general | solution.py:186
  (234 shorter events, 97.5 us)
Async XLA Ops:
  8.0 414.4 %copy-start = (bf16[2048,512]{1,0:T(8,128)(2,1)S(1)}, bf16[2048,512]{1,0:T(8,128)(2,1)}, u32[]{:S(2)}) copy-start(bf16[2048,512]{1,0:T(8,128)(2,1)} %param.45) | copy-start | bytes 6291460
  8.0 32.7 %copy-start.8 = (bf16[2,128,1,512]{3,1,2,0:T(8,128)(2,1)S(1)}, bf16[2,128,1,512]{3,1,2,0:T(8,128)(2,1)}, u32[]{:S(2)}) copy-start(bf16[2,128,1,512]{3,1,2,0:T(8,128)(2,1)} %param.26) | copy-start | bytes 786436
  8.0 32.7 %copy-start.3 = (bf16[2,128,2048]{2,1,0:T(8,128)(2,1)S(1)}, bf16[2,128,2048]{2,1,0:T(8,128)(2,1)}, u32[]{:S(2)}) copy-start(bf16[2,128,2048]{2,1,0:T(8,128)(2,1)} %param.24) | copy-start | bytes 3145732
  9.7 30.2 %collective-permute-start = (bf16[2,3,2560]{2,1,0:T(4,128)(2,1)}, bf16[2,3,2560]{2,1,0:T(4,128)(2,1)}, u32[]{:S(2)}, u32[]{:S(2)}) collective-permute-start(bf16[2,3,2560]{2,1,0:T(4,128)(2,1)} %pad_maximum_fusion.3), channel_id=1, source_target_pairs={{0,8},{8,16},{16,24},{24,32},{32,40},{40,48},{48,56},{56,64},{64,7... | collective-permute-start | bytes 92168 | tf_op jit(solution)/shard_map/ppermute | solution.py:20
  19.3 19.1 %all-to-all-start = ((f32[16,2,1,32]{3,1,2,0:T(2,128)}), f32[16,2,1,32]{3,1,2,0:T(2,128)}, u32[]{:S(2)}, u32[]{:S(2)}) async-start(f32[16,2,1,32]{3,1,2,0:T(2,128)} %broadcast_in_dim.46), calls=%async_computation | async-start | bytes 32768 | tf_op jit(solution)/shard_map/all_to_all | solution.py:46
  25.5 174.7 %all-reduce.2.cloned.1.call-start = ((), (), s32[]{:S(2)}) async-start(), calls=%async_computation.4 | async-start | bytes 8511488 | tf_op jit(solution)/shard_map/psum | solution.py:73
  62.1 177.3 %all-gather.14.cloned.1.call-start = ((), (), s32[]{:S(2)}) async-start(), calls=%async_computation.6 | async-start | bytes 12582912 | tf_op jit(solution)/shard_map/all_gather | solution.py:34
  62.1 141.0 %copy-start.50 = (s32[8]{0:T(128)S(1)}, s32[8]{0:T(128)}, u32[]{:S(2)}) copy-start(s32[8]{0:T(128)} %param.44) | copy-start | bytes 100
  62.7 324.0 %all-gather.8.cloned.1.call-start = ((), (), s32[]{:S(2)}) async-start(), calls=%async_computation.2 | async-start | bytes 12582912 | tf_op jit(solution)/shard_map/all_gather | solution.py:34
  245.5 176.9 %all-gather.12.cloned.1.call-start = ((), (), s32[]{:S(2)}) async-start(), calls=%async_computation.5 | async-start | bytes 2228224 | tf_op jit(solution)/shard_map/all_gather | solution.py:242
  273.1 28.2 %copy-start.33 = (f32[8,256,1,1]{1,0,2,3:T(8,128)S(1)}, f32[8,256,1,1]{1,0,2,3:T(8,128)}, u32[]{:S(2)}) copy-start(f32[8,256,1,1]{1,0,2,3:T(8,128)} %get-tuple-element.139) | copy-start | bytes 24580
  301.3 28.4 %copy-start.32 = (f32[8,256,1,1]{1,0,2,3:T(8,128)S(1)}, f32[8,256,1,1]{1,0,2,3:T(8,128)}, u32[]{:S(2)}) copy-start(f32[8,256,1,1]{1,0,2,3:T(8,128)} %get-tuple-element.141) | copy-start | bytes 24580
  329.7 28.2 %copy-start.34 = (f32[8,256,1,1]{1,0,2,3:T(8,128)S(1)}, f32[8,256,1,1]{1,0,2,3:T(8,128)}, u32[]{:S(2)}) copy-start(f32[8,256,1,1]{1,0,2,3:T(8,128)} %get-tuple-element.143) | copy-start | bytes 24580
  358.0 27.9 %copy-start.10 = (bf16[4,8,2048]{2,1,0:T(8,128)(2,1)S(1)}, bf16[4,8,2048]{2,1,0:T(8,128)(2,1)}, u32[]{:S(2)}) copy-start(bf16[4,8,2048]{2,1,0:T(8,128)(2,1)} %param.41) | copy-start | bytes 393220
  358.0 28.7 %copy-start.42 = (f32[2,1,32,1]{2,3,1,0:T(1,128)S(1)}, f32[2,1,32,1]{2,3,1,0:T(1,128)}, u32[]{:S(2)}) copy-start(f32[2,1,32,1]{2,3,1,0:T(1,128)} %copy-done.41) | copy-start | bytes 772
  358.0 28.7 %copy-start.47 = (f32[2,32]{1,0:T(2,128)S(1)}, f32[2,32]{1,0:T(2,128)}, u32[]{:S(2)}) copy-start(f32[2,32]{1,0:T(2,128)} %get-tuple-element.158) | copy-start | bytes 772
  386.6 190.8 %all-gather.10.cloned.1.call-start = ((), (), s32[]{:S(2)}) async-start(), calls=%async_computation.3 | async-start | bytes 20971520 | tf_op jit(solution)/shard_map/all_gather | solution.py:34
  426.3 23.9 %all-to-all-start.1 = ((f32[8,4,16,512]{3,2,1,0:T(8,128)}), f32[8,4,16,512]{3,2,1,0:T(8,128)S(1)}, u32[]{:S(2)}, u32[]{:S(2)}) async-start(f32[8,4,16,512]{3,2,1,0:T(8,128)} %copy.143), calls=%async_computation.1 | async-start | bytes 2097152 | tf_op jit(solution)/shard_map/all_to_all | solution.py:85
  432.8 144.7 %copy-start.40 = (f32[2,1,32,1]{2,3,1,0:T(1,128)S(1)}, f32[2,1,32,1]{2,3,1,0:T(1,128)}, u32[]{:S(2)}) copy-start(f32[2,1,32,1]{2,3,1,0:T(1,128)} %copy-done.39) | copy-start | bytes 772
  432.8 144.6 %copy-start.46 = (f32[2,32]{1,0:T(2,128)S(1)}, f32[2,32]{1,0:T(2,128)}, u32[]{:S(2)}) copy-start(f32[2,32]{1,0:T(2,128)} %get-tuple-element.157) | copy-start | bytes 772
  432.8 144.6 %copy-start.51 = (f32[2,32]{1,0:T(2,128)S(1)}, f32[2,32]{1,0:T(2,128)}, u32[]{:S(2)}) copy-start(f32[2,32]{1,0:T(2,128)} %get-tuple-element.107) | copy-start | bytes 772
  432.8 144.6 %copy-start.52 = (f32[2,32]{1,0:T(2,128)S(1)}, f32[2,32]{1,0:T(2,128)}, u32[]{:S(2)}) copy-start(f32[2,32]{1,0:T(2,128)} %get-tuple-element.108) | copy-start | bytes 772
  432.8 144.6 %copy-start.53 = (f32[2,32]{1,0:T(2,128)S(1)}, f32[2,32]{1,0:T(2,128)}, u32[]{:S(2)}) copy-start(f32[2,32]{1,0:T(2,128)} %get-tuple-element.109) | copy-start | bytes 772
  432.9 144.6 %copy-start.54 = (f32[2,32]{1,0:T(2,128)S(1)}, f32[2,32]{1,0:T(2,128)}, u32[]{:S(2)}) copy-start(f32[2,32]{1,0:T(2,128)} %get-tuple-element.150) | copy-start | bytes 772
  (40 other events, 336.0 us)
Sparse Core Ops, SparseCore 0:
  62.2 137.9 all-reduce.1
Sparse Core Ops, SparseCore 1:
  64.2 24.1 all-gather.13
  245.6 107.3 all-gather.7
  386.7 35.6 all-gather.11
  424.1 153.3 all-gather.9
where the time goes:
time: 622 us; the launch traced here: 611 us
  waiting for transfers between devices  266 us (43%)
  matrix products  183 us (29%)
  local copies, waits for them, and re-layouts  63.3 us (10%)
  other arithmetic  49.9 us (8%)
  starting transfers between devices  17.5 us (3%)
  between operations  16.9 us (3%)
  blocking collectives  14.4 us (2%)
    all_gather x3, waiting for transfers between devices, carried_in(): pieces = jax.tree.map(lambda part: lax.all_gather(part, axis), subtotal)  127 us
    psum x1, waiting for transfers between devices, in_one(): subtotal = lax.psum(jnp.concatenate([a.ravel() for a in arrays]), axis)  110 us
    dot_general x4, matrix products, shards(): jnp.einsum('rghpn,rgn->rghp', state, row_mixers[..., state_size:], precis...  107 us
    all_gather x1, waiting for transfers between devices, shards(): lax.all_gather(dec_hidden, CTX, axis=1, tiled=True).reshape(-1, width)  27.6 us
    dot_general x1, matrix products, shards(): state = jnp.einsum('rs,sghpn->rghpn', pick, final, precision=highest)  26.9 us
    dot_general x1, matrix products, shards(): jnp.einsum('stgn,sghpn->stghp', c_part, entry_state, precision=highest)  18.4 us
    all_gather x3, blocking collectives, carried_in(): pieces = jax.tree.map(lambda part: lax.all_gather(part, axis), subtotal)  14.4 us
    dot_general x2, matrix products, local_mixing(): return jnp.einsum('ghtu,ughp->tghp', mixing, values_one, precision=highest)  13.4 us
  transfers between devices with their start and end apart: 8, of which 4 were waited for; matrix products, arithmetic and copies ran while one was open for 39% of the time, Pallas kernels for 0%

commit v1 on v0

v1 whole, which is shorter than its diff:
```python
import functools

import jax
import jax.numpy as jnp
from jax import lax
from jax.experimental import pallas as pl
from jax.experimental.pallas import tpu as pltpu
from jax.sharding import PartitionSpec as P

MESH = pl.DeviceIdType.MESH
F32, BF16 = jnp.float32, jnp.bfloat16
HIGH = lax.Precision.HIGHEST
LANES = 128
CHIPS, CTX, TP = 8, 16, 8


def split(v):
    high = v.astype(BF16)
    return high, (v - high.astype(F32)).astype(BF16)


def dot(a, b):
    return jnp.dot(a, b, preferred_element_type=F32)


def silu(v):
    return v / (1.0 + jnp.exp(-v))


def softplus(v):
    return jnp.maximum(v, 0.0) + jnp.log1p(jnp.exp(-jnp.abs(v)))


def kernel(
    x_ref, bc_ref, z_hbm, dt_ref, par_ref, pbc_ref, hp_ref, init_hbm, rim0_ref,
    dx_ref, dz_ref, dbc_ref, sm_ref, len_ref, w_hbm,
    pre_ref, lay_ref,
    zbuf, ibuf, wbuf, rimsend, rimrecv, rimf, tailx, tailbc,
    dxr, dzr, dbcr, smr, txr, tbr,
    runrows, cols, bthl, chl, scs, dall, drecv, dstage, dchip,
    osend, oown, orecv, ostage, arecv, est, retst, erecv, e2send, e2recv,
    vp, er, yacc, ssqp, gbuf, ssqs, ssqr, flat, fstage, rbuf,
    lsem, rims, rimr, decs, decr, d2s, d2r, dds, ddr, as_, ar, ads, adr,
    rs_, rr, e2s, e2r, gs, gr, gfs, gfr, qs, qr, ts, tr,
):
    c, t = lax.axis_index("ctx"), lax.axis_index("tp")
    q, core = lax.div(c, 2), lax.rem(c, 2)
    mate = q * 2 + (1 - core)
    blk = core * CHIPS + q
    prompts, tokens, width = x_ref.shape
    tiles = width // LANES
    states = init_hbm.shape[3]
    steps, batch = dx_ref.shape[:2]
    rows = batch * CTX

    def lanes_of(j, size=LANES):
        return pl.ds(pl.multiple_of(j * size, size), size)

    def remote(src, dst, ssem, rsem, ctx=None, tp=None):
        return pltpu.make_async_remote_copy(
            src_ref=src, dst_ref=dst, send_sem=ssem, recv_sem=rsem,
            device_id=(c if ctx is None else ctx, t if tp is None else tp),
            device_id_type=MESH,
        )

    zcopy = pltpu.make_async_copy(z_hbm, zbuf, lsem.at[0])
    icopy = pltpu.make_async_copy(init_hbm.at[:, blk], ibuf, lsem.at[1])
    wcopy = pltpu.make_async_copy(w_hbm, wbuf, lsem.at[2])
    zcopy.start()
    icopy.start()
    wcopy.start()

    ends = [x_ref[s, tokens - 16 :, :].astype(F32)[8:] for s in range(prompts)]
    rimsend[:, :width] = jnp.concatenate(ends, 0).astype(BF16)
    ends = [bc_ref[s, tokens - 16 :, :].astype(F32)[8:] for s in range(prompts)]
    rimsend[:, width:] = jnp.concatenate(ends, 0).astype(BF16)
    place = lax.broadcasted_iota(jnp.int32, (8, tokens), 1) + c * tokens
    slot = lax.broadcasted_iota(jnp.int32, (8, tokens), 0)
    tx, tbc = [], []
    for s in range(prompts):
        hit = (place == len_ref[s] - 3 + slot) & (slot < 3)
        pick = jnp.where(hit, 1.0, 0.0).astype(BF16)
        tx.append(dot(pick, x_ref[s]))
        tbc.append(dot(pick, bc_ref[s]))
    tailx[...] = jnp.concatenate(tx, 0).astype(BF16)
    tailbc[...] = jnp.concatenate(tbc, 0).astype(BF16)
    dxr[:, c] = dx_ref[:, :, lanes_of(blk)]
    dzr[:, c] = dz_ref[:, :, lanes_of(blk)]
    dbcr[:, c] = dbc_ref[...]
    smr[c] = sm_ref[...]
    txr[c] = tailx[:, lanes_of(blk)]
    tbr[c] = tailbc[...]
    dall[...] = jnp.zeros_like(dall)
    dstage[...] = jnp.zeros_like(dstage)

    barrier = pltpu.get_barrier_semaphore()
    for k in range(1, CTX):
        pl.semaphore_signal(barrier, inc=1, device_id=(lax.rem(c + k, CTX), t), device_id_type=MESH)
    for k in range(1, TP):
        pl.semaphore_signal(barrier, inc=1, device_id=(c, lax.rem(t + k, TP)), device_id_type=MESH)
    pl.semaphore_wait(barrier, CTX - 1 + TP - 1)

    rim = remote(rimsend, rimrecv, rims, rimr, ctx=lax.rem(c + 1, CTX))
    rim.start()

    def decode_copies(k, source):
        to = lax.rem(c + k, CTX)
        their = lax.rem(to, 2) * CHIPS + lax.div(to, 2)
        at = lax.rem(c + CTX - k, CTX) if source else c
        pairs = (
            (dx_ref.at[:, :, lanes_of(their)], dxr.at[:, at]),
            (dz_ref.at[:, :, lanes_of(their)], dzr.at[:, at]),
            (dbc_ref, dbcr.at[:, at]),
            (sm_ref, smr.at[at]),
            (tailx.at[:, lanes_of(their)], txr.at[at]),
            (tailbc, tbr.at[at]),
        )
        return [
            remote(src, dst, decs.at[i, k], decr.at[i, k], ctx=to)
            for i, (src, dst) in enumerate(pairs)
        ]

    @pl.loop(1, CTX)
    def _(k):
        for copy in decode_copies(k, False):
            copy.start()

    upto = lax.broadcasted_iota(jnp.int32, (tokens, tokens), 0)
    at_lane = lax.broadcasted_iota(jnp.int32, (tokens, tokens), 1)
    upper = jnp.where(upto <= at_lane, 1.0, 0.0)
    lower = upto >= at_lane
    heads = dt_ref.shape[1]
    lane_place = lax.broadcasted_iota(jnp.int32, (heads, tokens), 1) + c * tokens
    for s in range(prompts):
        live = lane_place < len_ref[s]
        step = jnp.where(live, softplus(dt_ref[s] + hp_ref[1]), 0.0)
        run = jnp.dot(-hp_ref[0] * step, upper, precision=HIGH, preferred_element_type=F32)
        runrows[s] = run
        both = jnp.concatenate([run, step, jnp.zeros((tokens - 2 * heads, tokens), F32)], 0)
        cols[s] = both.T

    rim.wait_recv()
    rimf[...] = jnp.where(c == 0, rim0_ref[...], rimrecv[...].astype(F32))

    def conv(rim_rows, body, taps):
        padded = jnp.concatenate([rim_rows, body], 0)
        total = taps[4:5]
        for k in range(4):
            total = total + taps[k : k + 1] * padded[5 + k : 5 + k + body.shape[0]]
        return silu(total)

    for s in range(prompts):
        act = conv(rimf[8 * s : 8 * s + 8, width:], bc_ref[s].astype(F32), pbc_ref[...])
        b, cc = act[:, :states], act[:, states:]
        bt = b.T
        high, low = split(bt)
        bthl[s] = jnp.concatenate([high, low], 1)
        chl[s] = jnp.concatenate(split(cc), 0)
        scores = jnp.dot(cc, bt, precision=HIGH, preferred_element_type=F32)
        scs[s] = jnp.where(lower, scores, 0.0)

    first_half = lax.broadcasted_iota(jnp.int32, (tokens, LANES), 1) < LANES // 2

    def columns(s, j):
        return pltpu.roll(cols[s], lax.rem(tokens - 2 * j, tokens), 1)

    def own_part(j, i, out):
        lanes = lanes_of(j)
        par = par_ref[:, lanes]
        for s in range(prompts):
            xv = conv(rimf[8 * s : 8 * s + 8, lanes], x_ref[s, :, lanes].astype(F32), par)
            col = columns(s, j)
            r = jnp.where(first_half, col[:, 0:1], col[:, 1:2])
            step = jnp.where(first_half, col[:, heads : heads + 1], col[:, heads + 1 : heads + 2])
            end = r[tokens - 1 : tokens]
            v = xv * step
            vp[s, j] = v
            er[s, j] = jnp.exp(r)
            yacc[s, j] = par[6:7] * xv
            dall[s : s + 1, lanes] = jnp.exp(end)
            high, low = split(v * jnp.exp(end - r))
            out[i, s] = dot(bthl[s], jnp.concatenate([high, high], 0)) + dot(
                bthl[s, :, :tokens], low
            )

    def chip_at(k):
        return lax.rem(q + k, CHIPS)

    @pl.loop(1, CHIPS + 1)
    def _(k):
        i = chip_at(k)
        own_part((1 - core) * CHIPS + i, i, osend)
        remote(osend.at[i], orecv.at[i], d2s.at[i], d2r.at[i], ctx=mate).start()

    half = CHIPS * LANES
    dsend = remote(dall.at[:, lanes_of(1 - core, half)], drecv, dds, ddr, ctx=mate)
    dsend.start()

    @pl.loop(1, CHIPS + 1)
    def _(k):
        i = chip_at(k)
        own_part(core * CHIPS + i, i, oown)

    dsend.wait_recv()
    is_first = core == 0

    def decays(s, i):
        own = dall[s : s + 1, lanes_of(core * CHIPS + i)]
        return own, drecv[s : s + 1, lanes_of(i)]

    @pl.loop(1, CHIPS + 1)
    def _(k):
        i = chip_at(k)
        remote(osend.at[i], orecv.at[i], d2s.at[i], d2r.at[i], ctx=mate).wait_recv()
        for s in range(prompts):
            down, theirs = decays(s, i)
            a = jnp.where(is_first, theirs, 1.0)
            b = jnp.where(is_first, 1.0, down)
            ostage[i, s] = (a * oown[i, s] + b * orecv[i, s]).astype(BF16)
            dstage[i, s : s + 1] = down * theirs

        @pl.when(k < CHIPS)
        def _():
            to = i * 2 + core
            remote(ostage.at[i], arecv.at[q], as_.at[k], ar.at[k], ctx=to).start()
            remote(dstage.at[i], dchip.at[q], ads.at[k], adr.at[k], ctx=to).start()

    arecv[q] = ostage[q]
    dchip[q] = dstage[q]

    @pl.loop(0, tiles)
    def _(j):
        for s in range(prompts):
            col = columns(s, j)
            mixing = []
            for h in range(2):
                row = runrows[s, pl.ds(2 * j + h, 1), :]
                gap = jnp.minimum(col[:, h : h + 1] - row, 0.0)
                mixing.append((jnp.exp(gap) * scs[s]).astype(BF16))
            both = jnp.concatenate(mixing, 1)
            v = vp[s, j]
            total = yacc[s, j]
            stacked = jnp.concatenate([jnp.where(first_half, v, 0.0), jnp.where(first_half, 0.0, v)], 0)
            for part in split(stacked):
                total = total + dot(both, part)
            yacc[s, j] = total

    icopy.wait()
    for s in range(prompts):
        est[s] = ibuf[s].T

    @pl.loop(0, CHIPS)
    def _(p):
        for s in range(prompts):
            retst[p, s] = est[s].astype(BF16)
        k = lax.rem(q - p + CHIPS, CHIPS)

        @pl.when(p != q)
        def _():
            back = lax.rem(p - q + CHIPS, CHIPS)
            to = p * 2 + core
            remote(retst.at[p], erecv.at[q], rs_.at[back], rr.at[back], ctx=to).start()
            remote(ostage.at[p], arecv.at[p], as_.at[k], ar.at[k], ctx=to).wait_recv()
            remote(dstage.at[p], dchip.at[p], ads.at[k], adr.at[k], ctx=to).wait_recv()

        for s in range(prompts):
            est[s] = dchip[p, s : s + 1] * est[s] + arecv[p, s].astype(F32)

    erecv[q] = retst[q]

    @pl.loop(1, CTX)
    def _(k):
        for copy in decode_copies(k, True):
            copy.wait_recv()

    par = par_ref[:, lanes_of(blk)]
    small = jnp.concatenate(
        [smr[:, i].reshape(rows, LANES) for i in range(2)], 1
    )
    second = small[:, LANES : LANES + 1] > 0.5
    rolled = pltpu.roll(small[:, :LANES], lax.rem(LANES - 2 * blk, LANES), 1)

    def total_of(ref, lanes):
        out = ref[0].astype(F32)
        for i in range(1, CTX):
            out = out + ref[i].astype(F32)
        return [jnp.where(second, out[8 + k : 9 + k], out[k : k + 1]) for k in range(3)]

    def flat_rows(ref, i):
        return ref[i].astype(F32).reshape(rows, ref.shape[3])

    seq_x = total_of(txr, LANES) + [flat_rows(dxr, i) for i in range(steps)]
    seq_b = total_of(tbr, 2 * states) + [flat_rows(dbcr, i) for i in range(steps)]

    def taps_on(seq, i, weights):
        total = weights[4:5]
        for k in range(4):
            total = total + weights[k : k + 1] * seq[i + k]
        return silu(total)

    final = [split(est[s]) for s in range(prompts)]
    bs, us, coefs = [], [], []
    grown = 1.0
    row8 = lax.broadcasted_iota(jnp.int32, (8, LANES), 0)
    squares = jnp.zeros((8, rows), F32)
    for i in range(steps):
        xd = taps_on(seq_x, i, par)
        bcd = taps_on(seq_b, i, pbc_ref[...])
        cd = bcd[:, states:]
        chigh, clow = split(cd)
        lane = first_half[:rows]
        step = jnp.where(lane, rolled[:, heads * i : heads * i + 1], rolled[:, heads * i + 1 : heads * i + 2])
        keep = jnp.exp(-par[7:8] * step)
        grown = grown * keep
        bs.append(bcd[:, :states])
        us = [keep * u for u in us] + [step * xd]
        y0 = [
            dot(chigh, high) + dot(clow, high) + dot(chigh, low) for high, low in final
        ]
        yd = grown * jnp.where(second, y0[1], y0[0]) + par[6:7] * xd
        for b, u in zip(bs, us):
            yd = yd + u * jnp.sum(b * cd, axis=1, keepdims=True)
        m = yd * silu(flat_rows(dzr, i))
        squares = squares + lax.dot_general(
            jnp.where(row8 == i, 1.0, 0.0), m * m, (((1,), (1,)), ((), ())),
            precision=HIGH, preferred_element_type=F32,
        )
        gbuf[lax.div(blk, 2), i * rows : (i + 1) * rows, lanes_of(lax.rem(blk, 2))] = (
            m * par[5:6]
        ).astype(BF16)
    ssqs[...] = squares
    ssqr[c] = squares

    def slab(chip, which):
        at = which * CHIPS + chip
        return gbuf.at[lax.div(at, 2), :, lanes_of(lax.rem(at, 2))]

    def gather_copy(k, source):
        at = lax.rem(q + CHIPS - k, CHIPS) if source else q
        to = lax.rem(q + k, CHIPS) * 2 + core
        return remote(slab(q, core), slab(at, core), gs.at[k], gr.at[k], ctx=to)

    def forward_copy(k, chip, source):
        which = 1 - core if source else core
        return remote(slab(chip, core), slab(chip, which), gfs.at[k], gfr.at[k], ctx=mate)

    def square_copy(k, source):
        at = lax.rem(c + CTX - k, CTX) if source else c
        return remote(ssqs, ssqr.at[at], qs.at[k], qr.at[k], ctx=lax.rem(c + k, CTX))

    forward_copy(0, q, False).start()

    @pl.loop(1, CHIPS)
    def _(k):
        gather_copy(k, False).start()

    @pl.loop(1, CTX)
    def _(k):
        square_copy(k, False).start()

    zcopy.wait()
    ssqp[...] = jnp.zeros_like(ssqp)

    def finish(s, j, entry):
        carried = dot(chl[s], entry)
        y = yacc[s, j] + (carried[:tokens] + carried[tokens:]) * er[s, j]
        m = y * silu(zbuf[s, :, lanes_of(j)].astype(F32))
        yacc[s, j] = m
        ssqp[s] += m * m

    @pl.loop(0, CHIPS)
    def _(k):
        i = lax.rem(q + CHIPS - k, CHIPS)

        @pl.when(k > 0)
        def _():
            remote(retst.at[i], erecv.at[i], rs_.at[k], rr.at[k], ctx=i * 2 + core).wait_recv()

        mine = []
        for s in range(prompts):
            down, theirs = decays(s, i)
            e = erecv[i, s].astype(F32)
            e2send[i, s] = jnp.where(is_first, down * e + oown[i, s], e).astype(BF16)
            mine.append(jnp.where(is_first, e, theirs * e + orecv[i, s]).astype(BF16))
        remote(e2send.at[i], e2recv.at[i], e2s.at[i], e2r.at[i], ctx=mate).start()
        for s in range(prompts):
            finish(s, core * CHIPS + i, mine[s])

    @pl.loop(0, CHIPS)
    def _(k):
        i = lax.rem(q + CHIPS - k, CHIPS)
        remote(e2send.at[i], e2recv.at[i], e2s.at[i], e2r.at[i], ctx=mate).wait_recv()
        for s in range(prompts):
            finish(s, (1 - core) * CHIPS + i, e2recv[i, s])

    @pl.loop(1, CHIPS)
    def _(k):
        gather_copy(k, True).wait_recv()
        forward_copy(k, lax.rem(q + CHIPS - k, CHIPS), False).start()

    for s in range(prompts):
        mean = jnp.sum(ssqp[s], axis=1, keepdims=True) * (1.0 / width)
        ssqp[s] = jnp.broadcast_to(lax.rsqrt(mean + 1e-5), ssqp.shape[1:])

    @pl.loop(0, tiles)
    def _(j):
        gain = par_ref[5:6, lanes_of(j)]
        for s in range(prompts):
            pre_ref[s, :, lanes_of(j)] = (yacc[s, j] * ssqp[s] * gain).astype(BF16)

    @pl.loop(0, CHIPS)
    def _(k):
        forward_copy(k, lax.rem(q + CHIPS - k, CHIPS), True).wait_recv()

    @pl.loop(1, CTX)
    def _(k):
        square_copy(k, True).wait_recv()

    wcopy.wait()
    squares = ssqr[0]
    for i in range(1, CTX):
        squares = squares + ssqr[i]
    scale = lax.rsqrt(squares * (1.0 / width) + 1e-5)
    scale = jnp.concatenate([scale, jnp.zeros((rows - 8, rows), F32)], 0).T
    pair = 2 * LANES
    flat[...] = dot(gbuf[0], wbuf[:pair, :])

    @pl.loop(1, CHIPS)
    def _(i):
        flat[...] += dot(gbuf[i], wbuf[pl.ds(pl.multiple_of(i * pair, pair), pair), :])

    for i in range(steps):
        fstage[i] = (flat[i * rows : (i + 1) * rows] * scale[:, i : i + 1]).astype(fstage.dtype)
    share = rows // TP

    def rows_of(at):
        return fstage.at[:, pl.ds(pl.multiple_of(at * share, share), share), :]

    def sum_copy(k, source):
        to = lax.rem(t + k, TP)
        at = lax.rem(t + TP - k, TP) if source else t
        return remote(rows_of(to), rbuf.at[at], ts.at[k], tr.at[k], tp=to)

    @pl.loop(1, TP)
    def _(k):
        sum_copy(k, False).start()

    rbuf[t] = fstage[:, pl.ds(pl.multiple_of(t * share, share), share), :]

    rim.wait_send()
    dsend.wait_send()
    forward_copy(0, q, False).wait_send()

    @pl.loop(1, CTX)
    def _(k):
        for copy in decode_copies(k, False):
            copy.wait_send()
        square_copy(k, False).wait_send()

    @pl.loop(0, CHIPS)
    def _(i):
        remote(osend.at[i], orecv.at[i], d2s.at[i], d2r.at[i], ctx=mate).wait_send()
        remote(e2send.at[i], e2recv.at[i], e2s.at[i], e2r.at[i], ctx=mate).wait_send()

    @pl.loop(1, CHIPS)
    def _(k):
        to = chip_at(k) * 2 + core
        remote(ostage.at[q], arecv.at[q], as_.at[k], ar.at[k], ctx=to).wait_send()
        remote(dstage.at[q], dchip.at[q], ads.at[k], adr.at[k], ctx=to).wait_send()
        remote(retst.at[q], erecv.at[q], rs_.at[k], rr.at[k], ctx=to).wait_send()
        gather_copy(k, False).wait_send()
        forward_copy(k, lax.rem(q + CHIPS - k, CHIPS), False).wait_send()

    @pl.loop(1, TP)
    def _(k):
        sum_copy(k, True).wait_recv()

    total = rbuf[0].astype(F32)
    for i in range(1, TP):
        total = total + rbuf[i].astype(F32)
    lay_ref[...] = total.astype(BF16)

    @pl.loop(1, TP)
    def _(k):
        sum_copy(k, False).wait_send()


def shards(
    inner_x, gate_z, proj_bc, dt_raw, a_log, dt_bias, d_skip, conv_x, conv_bc, bias_x, bias_bc,
    norm_gain, init_state, init_conv_x, init_conv_bc, lengths, dec_x, dec_z, dec_bc, dec_dt,
    row_prompt, w_out,
):
    prompts, tokens, width = inner_x.shape
    bc_width = proj_bc.shape[3]
    states = bc_width // 2
    heads = dt_raw.shape[1]
    head = width // heads
    steps, batch = dec_x.shape[:2]
    out_width = w_out.shape[1]
    tiles = width // LANES
    rows = batch * CTX
    rate = jnp.exp(a_log)

    def over(v):
        return jnp.repeat(v, head)[None]

    par = jnp.concatenate(
        [conv_x, bias_x[None], norm_gain[None], over(d_skip), over(rate)], 0
    )
    pbc = jnp.concatenate(
        [conv_bc.reshape(4, bc_width), bias_bc, jnp.zeros((3, bc_width), F32)], 0
    )
    hp = jnp.broadcast_to(jnp.stack([rate, dt_bias])[:, :, None], (2, heads, tokens))
    rim0 = jnp.concatenate([init_conv_x, init_conv_bc.reshape(prompts, 3, bc_width)], -1)
    rim0 = jnp.pad(rim0.astype(F32), ((0, 0), (5, 0), (0, 0))).reshape(8 * prompts, -1)
    stepd = softplus(dec_dt + dt_bias[None, :, None])
    stepd = jnp.transpose(stepd, (2, 0, 1)).reshape(batch, steps * heads)
    which = jnp.broadcast_to(row_prompt[:, None].astype(F32), (batch, LANES))
    small = jnp.stack([stepd, which])

    vm = pl.BlockSpec(memory_space=pltpu.VMEM)
    hb = pl.BlockSpec(memory_space=pltpu.HBM)
    sm = pl.BlockSpec(memory_space=pltpu.SMEM)
    dma = pltpu.SemaphoreType.DMA
    V = pltpu.VMEM
    state = (CHIPS, prompts, states, LANES)
    tile = (prompts, tiles, tokens, LANES)
    scratch = [
        V((prompts, tokens, width), BF16),
        V((prompts, LANES, states), F32),
        V((width, out_width), BF16),
        V((8 * prompts, width + bc_width), BF16),
        V((8 * prompts, width + bc_width), BF16),
        V((8 * prompts, width + bc_width), F32),
        V((8 * prompts, width), BF16),
        V((8 * prompts, bc_width), BF16),
        V((steps, CTX, batch, LANES), BF16),
        V((steps, CTX, batch, LANES), BF16),
        V((steps, CTX, batch, bc_width), BF16),
        V((CTX, 2, batch, LANES), F32),
        V((CTX, 8 * prompts, LANES), BF16),
        V((CTX, 8 * prompts, bc_width), BF16),
        V((prompts, heads, tokens), F32),
        V((prompts, tokens, tokens), F32),
        V((prompts, states, 2 * tokens), BF16),
        V((prompts, 2 * tokens, states), BF16),
        V((prompts, tokens, tokens), F32),
        V((8, width), F32),
        V((8, CHIPS * LANES), F32),
        V((CHIPS, 8, LANES), F32),
        V((CHIPS, 8, LANES), F32),
        V(state, F32),
        V(state, F32),
        V(state, F32),
        V(state, BF16),
        V(state, BF16),
        V((prompts, states, LANES), F32),
        V(state, BF16),
        V(state, BF16),
        V(state, BF16),
        V(state, BF16),
        V(tile, F32),
        V(tile, F32),
        V(tile, F32),
        V((prompts, tokens, LANES), F32),
        V((tiles // 2, steps * rows, 2 * LANES), BF16),
        V((8, rows), F32),
        V((CTX, 8, rows), F32),
        V((steps * rows, out_width), F32),
        V((steps, rows, out_width), F32),
        V((TP, steps, rows // TP, out_width), F32),
        dma((3,)),
        dma,
        dma,
        dma((6, CTX)),
        dma((6, CTX)),
        dma((CHIPS,)),
        dma((CHIPS,)),
        dma,
        dma,
        *[dma((CHIPS,)) for _ in range(12)],
        dma((CTX,)),
        dma((CTX,)),
        dma((TP,)),
        dma((TP,)),
    ]
    return pl.pallas_call(
        kernel,
        out_shape=(
            jax.ShapeDtypeStruct((prompts, tokens, width), BF16),
            jax.ShapeDtypeStruct((steps, rows // TP, out_width), BF16),
        ),
        in_specs=[vm, vm, hb, vm, vm, vm, vm, hb, vm, vm, vm, vm, vm, sm, hb],
        out_specs=(vm, vm),
        scratch_shapes=scratch,
        compiler_params=pltpu.CompilerParams(
            collective_id=0, has_side_effects=True, vmem_limit_bytes=60 * 2**20
        ),
        name="mixer",
    )(
        inner_x, proj_bc.reshape(prompts, tokens, bc_width), gate_z, dt_raw, par, pbc, hp,
        init_state.reshape(prompts, tiles, LANES, states), rim0, dec_x, dec_z,
        dec_bc.reshape(steps, batch, bc_width), small, lengths, w_out,
    )


def solution(mesh):
    ctx, tp = "ctx", "tp"
    placed = (
        P(None, ctx, tp), P(None, ctx, tp), P(None, ctx, tp, None), P(None, tp, ctx),
        P(tp), P(tp), P(tp), P(None, tp), P(None, tp, None), P(tp), P(tp, None), P(tp),
        P(None, tp, None, None), P(None, None, tp), P(None, None, tp, None), P(),
        P(None, ctx, tp), P(None, ctx, tp), P(None, ctx, tp, None), P(None, tp, ctx),
        P(ctx), P(tp, ctx),
    )
    return jax.shard_map(
        shards,
        mesh=mesh,
        in_specs=placed,
        out_specs=(P(None, ctx, tp), P(None, tp, ctx)),
        check_vma=False,
    )
```

time: 622 us -> 105 us (0.17); the launches traced: 611 us -> 103 us
  waiting for transfers between devices: 266 us -> 0 us
  matrix products: 183 us -> 0 us
  Pallas kernels: 0 us -> 88 us
  local copies, waits for them, and re-layouts: 63.3 us -> 9.16 us
  other arithmetic: 49.9 us -> 4.81 us
  starting transfers between devices: 17.5 us -> 0 us
  between operations: 16.9 us -> 0.66 us
  blocking collectives: 14.4 us -> 0 us
    dot_general x14 -> x0, matrix products: 183 us -> none  [the longest x4 107 us: shards(): jnp.einsum('rghpn,rgn->rghp', state, row_mixers[..., state_size:], precis...]
    all_gather x4 -> x0, waiting for transfers between devices: 154 us -> none  [the longest x3 127 us: carried_in(): pieces = jax.tree.map(lambda part: lax.all_gather(part, axis), subtotal)]
    psum x1 -> x0, waiting for transfers between devices: 110 us -> none  [in_one(): subtotal = lax.psum(jnp.concatenate([a.ravel() for a in arrays]), axis)]
    pallas_call x0 -> x1, Pallas kernels: none -> 88 us  [shards(): pl.pallas_call(kernel, out_shape=(jax.ShapeDtypeStruct((prompts, tokens,...]
    reshape x19 -> x1, local copies, waits for them, and re-layouts: 20.8 us -> 0.7 us  [shards(): jnp.pad(rim0.astype(F32), ((0, 0), (5, 0), (0, 0))).reshape(8 * prompts, -1)]
    slice x10 -> x0, local copies, waits for them, and re-layouts: 14.9 us -> none  [the longest x2 5.91 us: in_one(): subtotal[b:e].reshape(a.shape)]
    all_gather x3 -> x0, blocking collectives: 14.4 us -> none  [carried_in(): pieces = jax.tree.map(lambda part: lax.all_gather(part, axis), subtotal)]
    mul x15 -> x0, other arithmetic: 14.4 us -> none  [the longest x3 6.88 us: shards(): step_row[..., None] * row_values]
  transfers between devices with their start and end apart: 8 -> 0, of which waited for: 4 -> 0; matrix products, arithmetic and copies ran while one was open for 39% -> 0% of each run, Pallas kernels for 0% -> 0%
where the time goes in v1:
time: 105 us; the launch traced here: 103 us
  Pallas kernels  88 us (84%)
  local copies, waits for them, and re-layouts  9.16 us (9%)
  other arithmetic  4.81 us (5%)
    pallas_call x1, Pallas kernels, shards(): pl.pallas_call(kernel, out_shape=(jax.ShapeDtypeStruct((prompts, tokens,...  88 us
    unnamed x3, local copies, waits for them, and re-layouts  4.48 us

profile of v1, /device:TPU:1, one launch (start us, length us, event | category | flops | bytes accessed | tf_op | source)
XLA Modules:
  0.0 102.6 jit_solution(14148007982719894141)
XLA Ops:
  0.6 0.7 convert_element_type.7
  1.3 0.1 pad.14.clone
  1.4 0.7 exponential_bitcast_fusion
  2.0 0.7 pad_maximum_fusion.1
  2.7 0.1 stack_broadcast_in_dim.2
  2.8 0.7 copy.30
  3.5 1.3 %maximum_maximum_fusion.pbc_ref = f32[8,512]{1,0:T(8,128)} fusion(f32[1,512]{1,0:T(1,128)} %param.32, f32[4,512]{1,0:T(4,128)S(1)} %bitcast.21, f32[8]{0:T(128)S(1)} %pad.14.clone), kind=kLoop, calls=%fused_computation.6 | loop fusion | flops 8192 | bytes 26656 | tf_op jit(solution)/shard_map/concatenate | solution.py:510
  4.8 0.1 broadcast_in_dim.26
  4.9 0.1 broadcast_in_dim_reshape.7
  5.0 0.7 broadcast_in_dim.25
  5.7 0.1 broadcast_in_dim_reshape.6
  5.8 0.7 add_bitcast_fusion
  6.5 0.1 stack_reshape.3
  6.6 0.6 pad_maximum_fusion.sm_ref
  7.2 0.7 broadcast_in_dim.28.hp_ref
  7.9 1.5 %concatenate.9.par_ref = f32[8,2048]{1,0:T(8,128)} concatenate(f32[4,2048]{1,0:T(4,128)} %param.29, f32[1,2048]{1,0:T(1,128)} %bitcast.22, f32[1,2048]{1,0:T(1,128)} %bitcast.23, f32[1,2048]{1,0:T(1,128)S(1)} %broadcast_in_dim_reshape.6, f32[1,2048]{1,0:T(1,128)S(1)} %broadcast_in_dim_reshape.7), dimensions={0} | concatenate | bytes 131072 | tf_op jit(solution)/shard_map/concatenate | solution.py:507
  9.4 0.8 fusion.3
  10.2 0.7 copy.29
  10.9 88.0 %mixer.1 = (bf16[2,128,2048]{2,1,0:T(8,128)(2,1)}, bf16[4,16,512]{2,1,0:T(8,128)(2,1)}) custom-call(bf16[2,128,2048]{2,1,0:T(8,128)(2,1)} %x_ref.1, bf16[2,128,512]{2,1,0:T(8,128)(2,1)} %bitcast.19, bf16[2,128,2048]{2,1,0:T(8,128)(2,1)} %z_hbm.1, f32[2,32,128]{2,1,0:T(8,128)} %dt_ref.1, f32[8,2048]{1,0:T(8,128)} %concatenate.9.par_ref, ...), custom_call_target="tpu_custom_call" | custom-call | tf_op jit(solution)/shard_map/mixer/pallas_call | solution.py:587
  98.9 2.3 %copy.33 = bf16[2,128,2048]{2,1,0:T(8,128)(2,1)} copy(bf16[2,128,2048]{2,1,0:T(8,128)(2,1)} %get-tuple-element.6) | data formatting | bytes 2097152
  101.2 1.5 %copy.34 = bf16[4,16,512]{2,1,0:T(8,128)(2,1)} copy(bf16[4,16,512]{2,1,0:T(8,128)(2,1)} %get-tuple-element.7) | data formatting | bytes 131072
  (2 shorter events, 0.0 us)

commit v2 on v1

v2 whole, which is shorter than its diff:
```python
import functools

import jax
import jax.numpy as jnp
from jax import lax
from jax.experimental import pallas as pl
from jax.experimental.pallas import tpu as pltpu
from jax.sharding import PartitionSpec as P

MESH = pl.DeviceIdType.MESH
F32, BF16 = jnp.float32, jnp.bfloat16
HIGH = lax.Precision.HIGHEST
LANES = 128
CHIPS, CTX, TP, PAIRS = 8, 16, 8, 4
PARTS = 4
FINISH = (3, 3)


def split(v):
    high = v.astype(BF16)
    return high, (v - high.astype(F32)).astype(BF16)


def dot(a, b):
    return jnp.dot(a, b, preferred_element_type=F32)


def silu(v):
    return v / (1.0 + jnp.exp(-v))


def softplus(v):
    return jnp.maximum(v, 0.0) + jnp.log1p(jnp.exp(-jnp.abs(v)))


def kernel(
    x_hbm, bc_hbm, z_hbm, dt_ref, alog_ref, dtb_ref, dsk_ref, cx_ref, cbc_ref, bx_ref, bbc_ref,
    gain_ref, init_hbm, icx_ref, icbc_ref, len_ref, dx_hbm, dz_hbm, dbc_hbm, ddt_ref, rp_ref, w_hbm,
    pre_hbm, lay_ref,
    x_ref, bc_ref, dx_ref, dz_ref, dbc_ref, pre_ref,
    zbuf, ibuf, wbuf, rimsend, rimrecv, rimf, tailx, tailbc, small, spread4, hrow,
    dxr, dzr, dbcr, smr, txr, tbr,
    runrows, cols, bthl, chl, scs, dall, drecv, ydsend, ydrecv, dchip, zdsend, zdrecv,
    osend, oown, orecv, ysend, yrecv, ochip, zsend, zrecv, est, retst, erecv, yesend, yerecv,
    e2send, e2recv, emine,
    vp, er, yacc, ssqp, gbuf, ssqs, ssqr, flat, fstage, rbuf, lsem, sems,
):
    c, t = lax.axis_index("ctx"), lax.axis_index("tp")
    q, core = lax.div(c, 2), lax.rem(c, 2)
    mate = q * 2 + (1 - core)
    blk = core * CHIPS + q
    prompts, tokens, width = x_ref.shape
    tiles = width // LANES
    states = init_hbm.shape[3]
    steps, batch = dx_ref.shape[:2]
    rows = batch * CTX
    heads = dt_ref.shape[1]

    barrier = pltpu.get_barrier_semaphore()
    for k in range(1, CTX):
        pl.semaphore_signal(barrier, inc=1, device_id=(lax.rem(c + k, CTX), t), device_id_type=MESH)
    for k in range(1, TP):
        pl.semaphore_signal(barrier, inc=1, device_id=(c, lax.rem(t + k, TP)), device_id_type=MESH)

    def lanes_of(j, size=LANES):
        return pl.ds(pl.multiple_of(j * size, size), size)

    def remote(src, dst, ssem, rsem, ctx=None, tp=None):
        return pltpu.make_async_remote_copy(
            src_ref=src, dst_ref=dst, send_sem=ssem, recv_sem=rsem,
            device_id=(c if ctx is None else ctx, t if tp is None else tp),
            device_id_type=MESH,
        )

    zed, why = lax.div(q, 2), lax.rem(q, 2)
    neighbour = (2 * zed + 1 - why) * 2 + core

    def device_of(chip):
        return chip * 2 + core

    def zed_at(k):
        return lax.rem(zed + k, PAIRS)

    def zed_from(k):
        return lax.rem(zed + PAIRS - k, PAIRS)

    taken = []

    def new(count=None):
        base = sum(taken)
        taken.append(count or 1)
        return sems.at[base] if count is None else lambda k: sems.at[base + k]

    def wait_sent(sem, ref):
        remote(ref, ref, sem, sem, ctx=mate).wait_send()

    def wait_got(sem, ref):
        remote(ref, ref, sem, sem, ctx=mate).wait_recv()

    rims, rimr = new(), new()
    decs, decr = new(3), new(3)
    sps, spn, spr, psr = new(3), new(3), new(3), new(3)
    d2s, d2r, dds, ddr, e2s, e2r = new(), new(CHIPS), new(), new(), new(), new()
    yos, yor, yds, ydr = new(), new(PAIRS), new(), new()
    zos, zor, zds, zdr = new(), new(PAIRS), new(), new()
    rs_, rr, yes_, yer = new(), new(PAIRS), new(), new(PAIRS)
    gns, gqs, gfs = new(), new(), new()
    gnr, gzr, gqr, gfr, qr, tr = [new(PARTS) for _ in range(6)]
    qs, ts = new(), new()
    assert sum(taken) == sems.shape[0]

    def load(at, src, dst):
        copy = pltpu.make_async_copy(src, dst, lsem.at[at])
        copy.start()
        return copy

    xcopy, bcopy = load(0, x_hbm, x_ref), load(1, bc_hbm, bc_ref)
    dcopies = [
        load(2, dx_hbm, dx_ref), load(3, dz_hbm, dz_ref), load(4, dbc_hbm, dbc_ref)
    ]
    icopy = load(5, init_hbm.at[:, blk], ibuf)
    zcopy, wcopy = load(6, z_hbm, zbuf), load(7, w_hbm, wbuf)

    hrow[...] = jnp.zeros_like(hrow)
    hrow[0:1, :heads] = jnp.exp(alog_ref[...])
    hrow[1:2, :heads] = dtb_ref[...]
    hrow[2:3, :heads] = dsk_ref[...]
    spread4[...] = jnp.zeros_like(spread4)
    for i in range(steps):
        spread4[i, :, :heads] = softplus(ddt_ref[i] + hrow[1:2, :heads])
    small[0] = sum(
        spread4[i] if i == 0 else pltpu.roll(spread4[i], heads * i, 1) for i in range(steps)
    )
    which = jnp.zeros((batch, LANES), F32)
    row_at = lax.broadcasted_iota(jnp.int32, (batch, LANES), 0)
    for r in range(batch):
        which = jnp.where(row_at == r, rp_ref[r].astype(F32), which)
    small[1] = which

    upto = lax.broadcasted_iota(jnp.int32, (tokens, tokens), 0)
    at_lane = lax.broadcasted_iota(jnp.int32, (tokens, tokens), 1)
    upper = jnp.where(upto <= at_lane, 1.0, 0.0)
    lower = upto >= at_lane
    hcol = jnp.concatenate([hrow[...], jnp.zeros((LANES - 8, LANES), F32)], 0).T
    rate_col, bias_col = hcol[:heads, 0:1], hcol[:heads, 1:2]
    lane_place = lax.broadcasted_iota(jnp.int32, (heads, tokens), 1) + c * tokens
    for s in range(prompts):
        live = lane_place < len_ref[s]
        step = jnp.where(live, softplus(dt_ref[s] + bias_col), 0.0)
        run = jnp.dot(-rate_col * step, upper, precision=HIGH, preferred_element_type=F32)
        runrows[s] = run
        both = jnp.concatenate([run, step, jnp.zeros((tokens - 2 * heads, tokens), F32)], 0)
        cols[s] = both.T
    first_half = lax.broadcasted_iota(jnp.int32, (tokens, LANES), 1) < LANES // 2
    ends = [cols[s][tokens - 1 :] for s in range(prompts)]
    ends = jnp.exp(jnp.concatenate(ends + [jnp.zeros((8 - prompts, LANES), F32)], 0))
    for j in range(tiles):
        dall[j] = jnp.where(first_half[:8], ends[:, 2 * j : 2 * j + 1], ends[:, 2 * j + 1 : 2 * j + 2])

    xcopy.wait()
    bcopy.wait()
    ends = [x_ref[s, tokens - 16 :, :].astype(F32)[8:] for s in range(prompts)]
    rimsend[:, :width] = jnp.concatenate(ends, 0).astype(BF16)
    ends = [bc_ref[s, tokens - 16 :, :].astype(F32)[8:] for s in range(prompts)]
    rimsend[:, width:] = jnp.concatenate(ends, 0).astype(BF16)
    pl.semaphore_wait(barrier, CTX - 1 + TP - 1)

    rim = remote(rimsend, rimrecv, rims, rimr, ctx=lax.rem(c + 1, CTX))
    pl.when(c != CTX - 1)(rim.start)
    half = pl.ds(pl.multiple_of((1 - core) * CHIPS, CHIPS), CHIPS)
    remote(dall.at[half], drecv, dds, ddr, ctx=mate).start()

    place = lax.broadcasted_iota(jnp.int32, (8, tokens), 1) + c * tokens
    slot = lax.broadcasted_iota(jnp.int32, (8, tokens), 0)
    tx, tbc = 0.0, 0.0
    for s in range(prompts):
        hit = (place == len_ref[s] - 3 + slot - 4 * s) & (slot >= 4 * s) & (slot < 4 * s + 3)
        pick = jnp.where(hit, 1.0, 0.0).astype(BF16)
        tx = tx + dot(pick, x_ref[s])
        tbc = tbc + dot(pick, bc_ref[s])
    tailx[...] = tx.astype(BF16)
    tailbc[...] = tbc.astype(BF16)

    for copy in dcopies:
        copy.wait()
    dxr[:, c] = dx_ref[:, :, lanes_of(blk)]
    dzr[:, c] = dz_ref[:, :, lanes_of(blk)]
    dbcr[:, c] = dbc_ref[...]
    smr[c] = small[...]
    txr[c] = tailx[:, lanes_of(blk)]
    tbr[c] = tailbc[...]

    def scatter_copies(k, source):
        to = lax.rem(c + k, CTX)
        their = lax.rem(to, 2) * CHIPS + lax.div(to, 2)
        at = lax.rem(c + CTX - k, CTX) if source else c
        pairs = (
            (dx_ref.at[:, :, lanes_of(their)], dxr.at[:, at]),
            (dz_ref.at[:, :, lanes_of(their)], dzr.at[:, at]),
            (tailx.at[:, lanes_of(their)], txr.at[at]),
        )
        return [
            remote(src, dst, decs(i), decr(i), ctx=to)
            for i, (src, dst) in enumerate(pairs)
        ]

    spread_refs = (dbc_ref, small, tailbc)

    def spread_to(at):
        return dbcr.at[:, at], smr.at[at], tbr.at[at]

    def spread_copies(k, source):
        if isinstance(k, int):
            to, at = neighbour, neighbour
        else:
            to, at = device_of(2 * zed_at(k) + why), device_of(2 * zed_from(k) + why)
        return [
            remote(src, dst, sps(i), spn(i) if isinstance(k, int) else spr(i), ctx=to)
            for i, (src, dst) in enumerate(zip(spread_refs, spread_to(at if source else c)))
        ]

    def relay_copies(k, source):
        at = device_of(2 * (zed_from(k) if source else zed) + 1 - why)
        return [
            remote(ref, ref, sps(i), spr(i), ctx=device_of(2 * zed_at(k) + why))
            for i, ref in enumerate(spread_to(at))
        ]

    def pass_copies(chip, source):
        at = chip * 2 + (1 - core if source else core)
        return [
            remote(ref, ref, sps(i), psr(i), ctx=mate)
            for i, ref in enumerate(spread_to(at))
        ]

    @pl.loop(1, CTX)
    def _(k):
        for copy in scatter_copies(k, False):
            copy.start()

    for copy in spread_copies(0, False):
        copy.start()

    @pl.loop(1, PAIRS)
    def _(k):
        for copy in spread_copies(k, False):
            copy.start()

    def entry_copy(k, source):
        to = zed_at(k)
        src, at = (zed, zed_from(k)) if source else (to, zed)
        return remote(
            retst.at[src], erecv.at[at], rs_, rr(k), ctx=device_of(2 * to + why)
        )

    icopy.wait()
    for s in range(prompts):
        est[s] = ibuf[s].T
        retst[0, s] = est[s].astype(BF16)

    @pl.when(zed != 0)
    def _():
        entry_copy(PAIRS - zed, False).start()

    @pl.when(c != 0)
    def _():
        rim.wait_recv()
        rimf[...] = rimrecv[...].astype(F32)

    @pl.when(c == 0)
    def _():
        rimf[...] = jnp.zeros_like(rimf)
        for s in range(prompts):
            for k in range(3):
                at = 8 * s + 5 + k
                rimf[at : at + 1, :width] = icx_ref[k].astype(F32)[s : s + 1]
                rimf[at : at + 1, width:] = icbc_ref[k].astype(F32)[s : s + 1]

    def conv(rim_rows, body, taps, bias):
        padded = jnp.concatenate([rim_rows, body], 0)
        total = bias
        for k in range(4):
            total = total + taps[k] * padded[5 + k : 5 + k + body.shape[0]]
        return silu(total)

    bc_taps = [cbc_ref[k] for k in range(4)]
    for s in range(prompts):
        act = conv(rimf[8 * s : 8 * s + 8, width:], bc_ref[s].astype(F32), bc_taps, bbc_ref[...])
        b, cc = act[:, :states], act[:, states:]
        bt = b.T
        high, low = split(bt)
        bthl[s] = jnp.concatenate([high, low], 1)
        chl[s] = jnp.concatenate(split(cc), 0)
        scores = jnp.dot(cc, bt, precision=HIGH, preferred_element_type=F32)
        scs[s] = jnp.where(lower, scores, 0.0)

    def columns(s, j):
        return pltpu.roll(cols[s], lax.rem(tokens - 2 * j, tokens), 1)

    def per_lane(row, j):
        rolled = pltpu.roll(hrow[...], lax.rem(LANES - 2 * j, LANES), 1)[row : row + 1]
        return jnp.where(first_half[:1], rolled[:, 0:1], rolled[:, 1:2])

    def taps_of(lanes):
        taps = cx_ref[:, lanes]
        return [taps[k : k + 1] for k in range(4)]

    def own_part(j, i, out):
        lanes = lanes_of(j)
        taps, skip = taps_of(lanes), per_lane(2, j)
        for s in range(prompts):
            body = x_ref[s, :, lanes].astype(F32)
            xv = conv(rimf[8 * s : 8 * s + 8, lanes], body, taps, bx_ref[:, lanes])
            col = columns(s, j)
            r = jnp.where(first_half, col[:, 0:1], col[:, 1:2])
            step = jnp.where(first_half, col[:, heads : heads + 1], col[:, heads + 1 : heads + 2])
            end = r[tokens - 1 : tokens]
            v = xv * step
            vp[s, j] = v
            er[s, j] = jnp.exp(r)
            yacc[s, j] = skip * xv
            high, low = split(v * jnp.exp(end - r))
            out[i, s] = dot(bthl[s], jnp.concatenate([high, high], 0)) + dot(
                bthl[s, :, :tokens], low
            )

    is_first = core == 0

    def state_copy(i):
        return remote(osend.at[i], orecv.at[i], d2s, d2r(i), ctx=mate)

    def decays(s, i):
        return dall[core * CHIPS + i, s : s + 1], drecv[i, s : s + 1]

    def pair_copy(at):
        return remote(ysend.at[at], yrecv.at[at], yos, yor(at), ctx=neighbour)

    def zed_copy(k, source, refs, ssem, rsem):
        to = zed_at(k)
        src, at = (zed, zed_from(k)) if source else (to, zed)
        return remote(refs[0].at[src], refs[1].at[at], ssem, rsem, ctx=device_of(2 * to + why))

    def zed_state(k, source):
        return zed_copy(k, source, (zsend, zrecv), zos, zor(k))

    def zed_decay(k):
        return zed_copy(k, False, (zdsend, zdrecv), zds, zdr)

    def block_of(n):
        at = lax.rem(zed + n, PAIRS)
        return at, 2 * at + jnp.where(n <= PAIRS, 1 - why, why)

    is_low = why == 0

    def combine(n):
        at, i = block_of(n)
        state_copy(i).wait_recv()
        for s in range(prompts):
            down, theirs = decays(s, i)
            a = jnp.where(is_first, theirs, 1.0)
            b = jnp.where(is_first, 1.0, down)
            ochip[at, s] = a * oown[i, s] + b * orecv[i, s]

        @pl.when(n <= PAIRS)
        def _():
            for s in range(prompts):
                ysend[at, s] = ochip[at, s].astype(BF16)
            pair_copy(at).start()

    def quad(m):
        at = zed_at(m)
        pair_copy(at).wait_recv()
        for s in range(prompts):
            down, theirs = dchip[at, s : s + 1], ydrecv[at, s : s + 1]
            a = jnp.where(is_low, theirs, 1.0)
            b = jnp.where(is_low, 1.0, down)
            zsend[at, s] = a * ochip[at, s] + b * yrecv[at, s].astype(F32)

    def quad_send(m):
        quad(m)
        zed_state(m, False).start()

    wait_got(ddr, drecv)
    for at in range(PAIRS):
        for ref, i in ((dchip, 2 * at + why), (ydsend, 2 * at + 1 - why)):
            ref[at] = dall[core * CHIPS + i] * drecv[i]
    pair_decays = remote(ydsend, ydrecv, yds, ydr, ctx=neighbour)
    pair_decays.start()

    @pl.loop(1, CHIPS + 1)
    def _(n):
        i = block_of(n)[1]
        own_part((1 - core) * CHIPS + i, i, osend)
        own_part(core * CHIPS + i, i, oown)
        state_copy(i).start()

        @pl.when(n > 1)
        def _():
            combine(n - 1)

        @pl.when(n == 3)
        def _():
            for copy in spread_copies(0, True):
                copy.wait_recv()

            @pl.loop(1, PAIRS)
            def _(k):
                for copy in relay_copies(k, False):
                    copy.start()

            pair_decays.wait_recv()
            zdsend[...] = dchip[...] * ydrecv[...]

            @pl.loop(1, PAIRS)
            def _(k):
                zed_decay(k).start()

        @pl.when(n > PAIRS + 2)
        def _():
            quad_send(n - PAIRS - 2)

    combine(CHIPS)

    def inside(j):
        for s in range(prompts):
            col = columns(s, j)
            mixing = []
            for h in range(2):
                row = runrows[s, pl.ds(2 * j + h, 1), :]
                gap = jnp.minimum(col[:, h : h + 1] - row, 0.0)
                mixing.append((jnp.exp(gap) * scs[s]).astype(BF16))
            both = jnp.concatenate(mixing, 1)
            v = vp[s, j]
            total = yacc[s, j]
            stacked = jnp.concatenate([jnp.where(first_half, v, 0.0), jnp.where(first_half, 0.0, v)], 0)
            for part in split(stacked):
                total = total + dot(both, part)
            yacc[s, j] = total

    cuts = (0, 4, 8, 10)
    pl.loop(0, cuts[1])(inside)
    quad_send(PAIRS - 1)
    pl.loop(cuts[1], cuts[2])(inside)
    quad(PAIRS)
    zrecv[zed] = zsend[zed]
    zdrecv[zed] = zdsend[zed]

    for copy in pass_copies(q, False):
        copy.start()

    for i, ref in enumerate(spread_to(pl.ds(0, 2 * (PAIRS - 1)))):
        wait_got(spr(i), ref)

    @pl.loop(0, CHIPS)
    def _(chip):
        @pl.when(chip != q)
        def _():
            for copy in pass_copies(chip, False):
                copy.start()

    wait_got(zdr, zdrecv.at[: PAIRS - 1])

    @pl.loop(0, PAIRS)
    def _(p):
        @pl.when(p > 0)
        def _():
            for s in range(prompts):
                retst[p, s] = est[s].astype(BF16)

        @pl.when((p > 0) & (p != zed))
        def _():
            entry_copy(lax.rem(p - zed + PAIRS, PAIRS), False).start()

        @pl.when(p != zed)
        def _():
            zed_state(lax.rem(zed - p + PAIRS, PAIRS), True).wait_recv()

        for s in range(prompts):
            est[s] = zdrecv[p, s : s + 1] * est[s] + zrecv[p, s]

    erecv[zed] = retst[zed]

    def entry_to_neighbour(at):
        return remote(yesend.at[at], yerecv.at[at], yes_, yer(at), ctx=neighbour)

    def mate_copy(i):
        return remote(e2send.at[i], e2recv.at[i], e2s, e2r, ctx=mate)

    def for_cores(i, s, e):
        down, theirs = decays(s, i)
        e2send[i, s] = jnp.where(is_first, down * e + oown[i, s], e)
        emine[i, s] = jnp.where(is_first, e, theirs * e + orecv[i, s])

    def entry_step(at):
        i = 2 * at + why
        entries = []
        for s in range(prompts):
            down, theirs = dchip[at, s : s + 1], ydrecv[at, s : s + 1]
            e = erecv[at, s].astype(F32)
            yesend[at, s] = jnp.where(is_low, down * e + ochip[at, s], e).astype(BF16)
            entries.append(jnp.where(is_low, e, theirs * e + yrecv[at, s].astype(F32)))
        entry_to_neighbour(at).start()
        for s in range(prompts):
            for_cores(i, s, entries[s])
        mate_copy(i).start()

    entry_step(zed)

    others = (dxr.at[:, : CTX - 1], dzr.at[:, : CTX - 1], txr.at[: CTX - 1])
    for i, ref in enumerate(others):
        wait_got(decr(i), ref)
    for i, ref in enumerate(spread_to(pl.ds(0, CHIPS))):
        wait_got(psr(i), ref)

    part_steps = steps // PARTS
    part = part_steps * rows

    def slab(chip, which, h):
        at = which * CHIPS + chip
        return gbuf.at[lax.div(at, 2), h * part : (h + 1) * part, lanes_of(lax.rem(at, 2))]

    def to_neighbour(h, source):
        at = 2 * zed + (1 - why if source else why)
        return remote(slab(q, core, h), slab(at, core, h), gns, gnr(h), ctx=neighbour)

    def gather_copy(k, h, source):
        at = 2 * zed_from(k) + why if source else q
        to = device_of(2 * zed_at(k) + why)
        return remote(slab(q, core, h), slab(at, core, h), gns, gzr(h), ctx=to)

    def relay_copy(k, h, source):
        piece = slab(2 * (zed_from(k) if source else zed) + 1 - why, core, h)
        to = device_of(2 * zed_at(k) + why)
        return remote(piece, piece, gqs, gqr(h), ctx=to)

    def forward_copy(chip, h, source):
        piece = slab(chip, 1 - core if source else core, h)
        return remote(piece, piece, gfs, gfr(h), ctx=mate)

    def square_copy(k, h, source):
        at = lax.rem(c + CTX - k, CTX) if source else c
        to = lax.rem(c + k, CTX)
        return remote(ssqs.at[h], ssqr.at[h, at], qs, qr(h), ctx=to)

    def send_along(h):
        @pl.loop(1, PAIRS)
        def _(k):
            gather_copy(k, h, False).start()

    def send_rows(h):
        to_neighbour(h, False).start()
        if h == 0:
            send_along(h)
        forward_copy(q, h, False).start()

        @pl.loop(1, CTX)
        def _(k):
            square_copy(k, h, False).start()

    def relay_rows(h):
        to_neighbour(h, True).wait_recv()

        @pl.loop(1, PAIRS)
        def _(k):
            relay_copy(k, h, False).start()

        if h + 1 < PARTS:
            send_along(h + 1)
        forward_copy(2 * zed + 1 - why, h, False).start()

    lanes = lanes_of(blk)
    taps, bias, gain = taps_of(lanes), bx_ref[:, lanes], gain_ref[:, lanes]
    rate, skip = per_lane(0, blk), per_lane(2, blk)
    second = smr[:, 1].reshape(rows, LANES)[:, 0:1] > 0.5
    sizes = smr[:, 0].reshape(rows, LANES)
    rolled = pltpu.roll(sizes, lax.rem(LANES - 2 * blk, LANES), 1)

    def window(ref):
        out = ref[0].astype(F32)
        for i in range(1, CTX):
            out = out + ref[i].astype(F32)
        return [jnp.where(second, out[4 + k : 5 + k], out[k : k + 1]) for k in range(3)]

    def flat_rows(ref, i):
        return ref[i].astype(F32).reshape(rows, ref.shape[3])

    seq_x = window(txr) + [flat_rows(dxr, i) for i in range(steps)]
    seq_b = window(tbr) + [flat_rows(dbcr, i) for i in range(steps)]

    def taps_on(seq, i, weights, total):
        for k in range(4):
            total = total + weights[k] * seq[i + k]
        return silu(total)

    final = [split(est[s]) for s in range(prompts)]
    bs, us = [], []
    grown = 1.0
    row8 = lax.broadcasted_iota(jnp.int32, (8, LANES), 0)
    for i in range(steps):
        xd = taps_on(seq_x, i, taps, bias)
        bcd = taps_on(seq_b, i, bc_taps, bbc_ref[...])
        cd = bcd[:, states:]
        chigh, clow = split(cd)
        at = heads * i
        step = jnp.where(first_half, rolled[:, at : at + 1], rolled[:, at + 1 : at + 2])
        keep = jnp.exp(-rate * step)
        grown = grown * keep
        bs.append(bcd[:, :states])
        us = [keep * u for u in us] + [step * xd]
        y0 = [
            dot(chigh, high) + dot(clow, high) + dot(chigh, low) for high, low in final
        ]
        yd = grown * jnp.where(second, y0[1], y0[0]) + skip * xd
        for b, u in zip(bs, us):
            yd = yd + u * jnp.sum(b * cd, axis=1, keepdims=True)
        m = yd * silu(flat_rows(dzr, i))
        if i % part_steps == 0:
            squares = jnp.zeros((8, rows), F32)
        squares = squares + lax.dot_general(
            jnp.where(row8 == i, 1.0, 0.0), m * m, (((1,), (1,)), ((), ())),
            precision=HIGH, preferred_element_type=F32,
        )
        gbuf[lax.div(blk, 2), i * rows : (i + 1) * rows, lanes_of(lax.rem(blk, 2))] = (
            m * gain
        ).astype(BF16)
        if i % part_steps == part_steps - 1:
            ssqs[i // part_steps] = squares
            ssqr[i // part_steps, c] = squares
            send_rows(i // part_steps)

    pl.loop(cuts[2], cuts[3])(inside)
    for h in range(PARTS):
        relay_rows(h)
        if h + 1 < PAIRS:
            entry_copy(h + 1, True).wait_recv()
            entry_step(zed_from(h + 1))
            pl.loop(cuts[3] + 2 * h, cuts[3] + 2 * h + 2)(inside)

    zcopy.wait()
    ssqp[...] = jnp.zeros_like(ssqp)

    def finish(s, j, entry):
        high, low = split(entry)
        carried = dot(chl[s], high)
        carried = carried[:tokens] + carried[tokens:] + dot(chl[s, :tokens], low)
        y = yacc[s, j] + carried * er[s, j]
        m = y * silu(zbuf[s, :, lanes_of(j)].astype(F32))
        yacc[s, j] = m
        ssqp[s] += m * m

    def finish_mine(i):
        for s in range(prompts):
            finish(s, core * CHIPS + i, emine[i, s])

    def own_column():
        @pl.loop(0, PAIRS)
        def _(k):
            finish_mine(2 * zed_from(k) + why)

    def other_column():
        @pl.loop(0, PAIRS)
        def _(k):
            at = zed_from(k)
            i = 2 * at + 1 - why
            entry_to_neighbour(at).wait_recv()
            for s in range(prompts):
                for_cores(i, s, yerecv[at, s].astype(F32))
            mate_copy(i).start()
            finish_mine(i)

    def other_core():
        wait_got(e2r, e2recv)

        @pl.loop(0, CHIPS)
        def _(i):
            for s in range(prompts):
                finish(s, (1 - core) * CHIPS + i, e2recv[i, s])

    wcopy.wait()
    pair, groups = 2 * LANES, CHIPS // 2
    share = rows // TP

    def projected(which, h):
        total = 0.0
        for g in range(groups):
            at = which * groups + g
            w = wbuf[pl.ds(pl.multiple_of(at * pair, pair), pair), :]
            total = total + dot(gbuf[at, h * part : (h + 1) * part], w)
        return total

    def rows_of(at):
        return pl.ds(pl.multiple_of(at * share, share), share)

    def sum_copy(k, h, source):
        to = lax.rem(t + k, TP)
        at = lax.rem(t + TP - k, TP) if source else t
        these = slice(h * part_steps, (h + 1) * part_steps)
        return remote(
            fstage.at[these, rows_of(to), :], rbuf.at[at, these], ts, tr(h), tp=to
        )

    for h in range(PARTS):

        three = gbuf.at[0, : (PAIRS - 1) * part // 2]
        wait_got(gzr(h), three)

        @pl.loop(1, PAIRS)
        def _(k):
            forward_copy(2 * zed_from(k) + why, h, False).start()

        wait_got(gqr(h), three)

        @pl.loop(1, PAIRS)
        def _(k):
            forward_copy(2 * zed_from(k) + 1 - why, h, False).start()

        flat[...] = projected(core, h)

        if h == 0:
            own_column()
        wait_got(gfr(h), gbuf.at[0])
        wait_got(qr(h), ssqr.at[h, : CTX - 1])

        squares = ssqr[h, 0]
        for i in range(1, CTX):
            squares = squares + ssqr[h, i]
        scale = lax.rsqrt(squares * (1.0 / width) + 1e-5)
        scale = jnp.concatenate([scale, jnp.zeros((rows - 8, rows), F32)], 0).T
        total = flat[...] + projected(1 - core, h)
        for i in range(part_steps):
            at = h * part_steps + i
            fstage[at] = (total[i * rows : (i + 1) * rows] * scale[:, at : at + 1]).astype(BF16)

        @pl.loop(1, TP)
        def _(k):
            sum_copy(k, h, False).start()

        if h == FINISH[0]:
            other_column()
        if h == FINISH[1]:
            other_core()

    rbuf[t] = fstage[:, rows_of(t), :]

    for s in range(prompts):
        mean = jnp.sum(ssqp[s], axis=1, keepdims=True) * (1.0 / width)
        ssqp[s] = jnp.broadcast_to(lax.rsqrt(mean + 1e-5), ssqp.shape[1:])

    outs = []
    for s in range(prompts):

        @pl.loop(0, tiles)
        def _(j):
            gain = gain_ref[:, lanes_of(j)]
            pre_ref[s, :, lanes_of(j)] = (yacc[s, j] * ssqp[s] * gain).astype(BF16)

        outs.append(pltpu.make_async_copy(pre_ref.at[s], pre_hbm.at[s], lsem.at[s]))
        outs[s].start()

    pl.when(c != CTX - 1)(rim.wait_send)
    wait_sent(dds, drecv)

    for i, ref in enumerate(others):
        wait_sent(decs(i), ref)
    for i, ref in enumerate(spread_to(pl.ds(0, CTX - 1))):
        wait_sent(sps(i), ref)
    three = slice(0, PAIRS - 1)
    for sem, ref in (
        (d2s, osend), (e2s, e2send), (yos, ysend), (yds, ydsend), (yes_, yesend),
        (zos, zsend.at[three]), (zds, zdsend.at[three]), (rs_, retst.at[three]),
        (gns, gbuf.at[:2]), (gqs, gbuf.at[three, : steps * rows // 2]), (gfs, gbuf.at[:4]),
        (qs, ssqr.at[:, : CTX - 1]),
    ):
        wait_sent(sem, ref)

    for h in range(PARTS):
        wait_got(tr(h), rbuf.at[: TP - 1, h * part_steps : (h + 1) * part_steps])

    total = rbuf[0].astype(F32)
    for i in range(1, TP):
        total = total + rbuf[i].astype(F32)
    lay_ref[...] = total.astype(BF16)

    wait_sent(ts, rbuf.at[: TP - 1])

    for copy in outs:
        copy.wait()


def hand_on(a_hbm, b_hbm, a_out, b_out, abuf, bbuf, isem, osem):
    pieces = [(b_hbm, bbuf, b_out)]
    half = a_hbm.shape[1] // 2
    for s in range(a_hbm.shape[0]):
        for r in range(2):
            at = (s, slice(r * half, (r + 1) * half))
            pieces.append((a_hbm.at[at], abuf.at[at], a_out.at[at]))
    into = [pltpu.make_async_copy(a, b, isem.at[i]) for i, (a, b, _) in enumerate(pieces)]
    out = [pltpu.make_async_copy(b, o, osem.at[i]) for i, (_, b, o) in enumerate(pieces)]
    for copy in into:
        copy.start()
    for first, then in zip(into, out):
        first.wait()
        then.start()
    for copy in out:
        copy.wait()


def shards(
    inner_x, gate_z, proj_bc, dt_raw, a_log, dt_bias, d_skip, conv_x, conv_bc, bias_x, bias_bc,
    norm_gain, init_state, init_conv_x, init_conv_bc, lengths, dec_x, dec_z, dec_bc, dec_dt,
    row_prompt, w_out,
):
    prompts, tokens, width = inner_x.shape
    bc_width = proj_bc.shape[3]
    states = bc_width // 2
    heads = dt_raw.shape[1]
    steps, batch = dec_x.shape[:2]
    out_width = w_out.shape[1]
    tiles = width // LANES
    rows = batch * CTX
    vm = pl.BlockSpec(memory_space=pltpu.VMEM)
    hb = pl.BlockSpec(memory_space=pltpu.HBM)
    sm = pl.BlockSpec(memory_space=pltpu.SMEM)
    dma = pltpu.SemaphoreType.DMA
    V = pltpu.VMEM
    state = (CHIPS, prompts, states, LANES)
    pairs = (PAIRS, prompts, states, LANES)
    tile = (prompts, tiles, tokens, LANES)
    scratch = [
        V((prompts, tokens, width), BF16),
        V((prompts, tokens, bc_width), BF16),
        V((steps, batch, width), BF16),
        V((steps, batch, width), BF16),
        V((steps, batch, bc_width), BF16),
        V((prompts, tokens, width), BF16),
        V((prompts, tokens, width), BF16),
        V((prompts, LANES, states), F32),
        V((width, out_width), BF16),
        V((8 * prompts, width + bc_width), BF16),
        V((8 * prompts, width + bc_width), BF16),
        V((8 * prompts, width + bc_width), F32),
        V((8, width), BF16),
        V((8, bc_width), BF16),
        V((2, batch, LANES), F32),
        V((steps, batch, LANES), F32),
        V((8, LANES), F32),
        V((steps, CTX, batch, LANES), BF16),
        V((steps, CTX, batch, LANES), BF16),
        V((steps, CTX, batch, bc_width), BF16),
        V((CTX, 2, batch, LANES), F32),
        V((CTX, 8, LANES), BF16),
        V((CTX, 8, bc_width), BF16),
        V((prompts, heads, tokens), F32),
        V((prompts, tokens, tokens), F32),
        V((prompts, states, 2 * tokens), BF16),
        V((prompts, 2 * tokens, states), BF16),
        V((prompts, tokens, tokens), F32),
        V((tiles, 8, LANES), F32),
        V((CHIPS, 8, LANES), F32),
        *[V((PAIRS, 8, LANES), F32) for _ in range(5)],
        V(state, F32),
        V(state, F32),
        V(state, F32),
        V(pairs, BF16),
        V(pairs, BF16),
        V(pairs, F32),
        V(pairs, F32),
        V(pairs, F32),
        V((prompts, states, LANES), F32),
        V(pairs, BF16),
        V(pairs, BF16),
        V(pairs, BF16),
        V(pairs, BF16),
        V(state, F32),
        V(state, F32),
        V(state, F32),
        V(tile, F32),
        V(tile, F32),
        V(tile, F32),
        V((prompts, tokens, LANES), F32),
        V((tiles // 2, steps * rows, 2 * LANES), BF16),
        V((PARTS, 8, rows), F32),
        V((PARTS, CTX, 8, rows), F32),
        V((steps * rows // PARTS, out_width), F32),
        V((steps, rows, out_width), BF16),
        V((TP, steps, rows // TP, out_width), BF16),
        dma((8,)),
        dma((86,)),
    ]
    prefill, layer = pl.pallas_call(
        kernel,
        out_shape=(
            jax.ShapeDtypeStruct((prompts, tokens, width), BF16),
            jax.ShapeDtypeStruct((steps, rows // TP, out_width), BF16),
        ),
        in_specs=[hb, hb, hb, *[vm] * 9, hb, vm, vm, sm, hb, hb, hb, vm, sm, hb],
        out_specs=(hb, vm),
        scratch_shapes=scratch,
        compiler_params=pltpu.CompilerParams(
            collective_id=0, has_side_effects=True, vmem_limit_bytes=60 * 2**20
        ),
        name="mixer",
    )(
        inner_x, proj_bc.reshape(prompts, tokens, bc_width), gate_z, dt_raw,
        a_log[None], dt_bias[None], d_skip[None], conv_x, conv_bc, bias_x[None], bias_bc,
        norm_gain[None], init_state.reshape(prompts, tiles, LANES, states),
        jnp.transpose(init_conv_x, (1, 0, 2)),
        jnp.transpose(init_conv_bc, (1, 2, 0, 3)).reshape(3, prompts, bc_width),
        lengths, dec_x, dec_z, dec_bc.reshape(steps, batch, bc_width),
        jnp.transpose(dec_dt, (0, 2, 1)), row_prompt, w_out,
    )
    halves = (prompts, tokens, width), (steps, rows // TP, out_width)
    return pl.pallas_call(
        hand_on,
        out_shape=tuple(jax.ShapeDtypeStruct(shape, BF16) for shape in halves),
        in_specs=[hb, hb],
        out_specs=(hb, hb),
        scratch_shapes=[*[V(shape, BF16) for shape in halves], dma((5,)), dma((5,))],
        name="results",
    )(prefill, layer)


def solution(mesh):
    ctx, tp = "ctx", "tp"
    placed = (
        P(None, ctx, tp), P(None, ctx, tp), P(None, ctx, tp, None), P(None, tp, ctx),
        P(tp), P(tp), P(tp), P(None, tp), P(None, tp, None), P(tp), P(tp, None), P(tp),
        P(None, tp, None, None), P(None, None, tp), P(None, None, tp, None), P(),
        P(None, ctx, tp), P(None, ctx, tp), P(None, ctx, tp, None), P(None, tp, ctx),
        P(ctx), P(tp, ctx),
    )
    return jax.shard_map(
        shards,
        mesh=mesh,
        in_specs=placed,
        out_specs=(P(None, ctx, tp), P(None, tp, ctx)),
        check_vma=False,
    )
```

time: 105 us -> 67.9 us (0.65); the launches traced: 103 us -> 67.7 us
  Pallas kernels: 88 us -> 67.1 us
  local copies, waits for them, and re-layouts: 9.16 us -> 0 us
  other arithmetic: 4.81 us -> 0 us
    pallas_call x1, Pallas kernels: 88 us -> 65 us  [shards(): pl.pallas_call(kernel, out_shape=(jax.ShapeDtypeStruct((prompts, tokens,...]
    unnamed x3 -> x0, local copies, waits for them, and re-layouts: 4.48 us -> none
    pallas_call x0 -> x1, Pallas kernels: none -> 2.04 us  [shards(): pl.pallas_call(hand_on, out_shape=tuple((jax.ShapeDtypeStruct(shape, BF16...]
    concatenate x2 -> x0, local copies, waits for them, and re-layouts: 1.54 us -> none  [the longest x1 1.46 us: shards(): jnp.concatenate([conv_x, bias_x[None], norm_gain[None], over(d_skip), ove...]
    broadcast_in_dim x4 -> x0, local copies, waits for them, and re-layouts: 1.48 us -> none  [the longest x2 0.8 us: over(): return jnp.repeat(v, head)[None]]
    concatenate x1 -> x0, other arithmetic: 1.35 us -> none  [shards(): jnp.concatenate([conv_bc.reshape(4, bc_width), bias_bc, jnp.zeros((3, bc_...]
    another operation x2 -> x0, other arithmetic: 1.27 us -> none  [the longest x1 0.67 us: shards(): jnp.stack([rate, dt_bias])[:, :, None]]
where the time goes in v2:
time: 67.9 us; the launch traced here: 67.7 us
  Pallas kernels  67.1 us (99%)
    pallas_call x1, Pallas kernels, shards(): pl.pallas_call(kernel, out_shape=(jax.ShapeDtypeStruct((prompts, tokens,...  65 us
    pallas_call x1, Pallas kernels, shards(): pl.pallas_call(hand_on, out_shape=tuple((jax.ShapeDtypeStruct(shape, BF16...  2.04 us

profile of v2, /device:TPU:1, one launch (start us, length us, event | category | flops | bytes accessed | tf_op | source)
XLA Modules:
  0.0 67.7 jit_solution(7362155663637568574)
XLA Ops:
  0.6 65.0 %mixer.1 = (bf16[2,128,2048]{2,1,0:T(8,128)(2,1)}, bf16[4,16,512]{2,1,0:T(8,128)(2,1)}) custom-call(bf16[2,128,2048]{2,1,0:T(8,128)(2,1)} %x_hbm.1, bf16[2,128,512]{2,1,0:T(8,128)(2,1)} %bitcast.16, bf16[2,128,2048]{2,1,0:T(8,128)(2,1)} %z_hbm.1, f32[2,32,128]{2,1,0:T(8,128)} %dt_ref.1, f32[1,32]{1,0:T(1,128)} %bitcast.23, f32[1,32]{1,0:T(1,128)} %bitcast.24, ...), custom_call_target="tpu_custom_call" | custom-call | tf_op jit(solution)/shard_map/mixer/pallas_call | solution.py:890
  65.7 2.0 %results.1 = (bf16[2,128,2048]{2,1,0:T(8,128)(2,1)}, bf16[4,16,512]{2,1,0:T(8,128)(2,1)}) custom-call(bf16[2,128,2048]{2,1,0:T(8,128)(2,1)} %get-tuple-element.4.a_hbm, bf16[4,16,512]{2,1,0:T(8,128)(2,1)} %get-tuple-element.5.b_hbm), custom_call_target="tpu_custom_call" | custom-call | tf_op jit(solution)/shard_map/results/pallas_call | solution.py:913

commit v3 on v2

--- a/solution.py
+++ b/solution.py
@@ -100,7 +100,7 @@
     rims, rimr = new(), new()
     decs, decr = new(3), new(3)
     sps, spn, spr, psr = new(3), new(3), new(3), new(3)
-    d2s, d2r, dds, ddr, e2s, e2r = new(), new(CHIPS), new(), new(), new(), new()
+    d2s, d2r, dds, ddr, e2s, e2r = new(), new(CHIPS), new(), new(), new(), new(2)
     yos, yor, yds, ydr = new(), new(PAIRS), new(), new()
     zos, zor, zds, zdr = new(), new(PAIRS), new(), new()
     rs_, rr, yes_, yer = new(), new(PAIRS), new(), new(PAIRS)
@@ -374,7 +374,7 @@
             down, theirs = dchip[at, s : s + 1], ydrecv[at, s : s + 1]
             a = jnp.where(is_low, theirs, 1.0)
             b = jnp.where(is_low, 1.0, down)
-            zsend[at, s] = a * ochip[at, s] + b * yrecv[at, s].astype(F32)
+            zsend[at, s] = (a * ochip[at, s] + b * yrecv[at, s].astype(F32)).astype(BF16)
 
     def quad_send(m):
         quad(m)
@@ -476,15 +476,15 @@
             zed_state(lax.rem(zed - p + PAIRS, PAIRS), True).wait_recv()
 
         for s in range(prompts):
-            est[s] = zdrecv[p, s : s + 1] * est[s] + zrecv[p, s]
+            est[s] = zdrecv[p, s : s + 1] * est[s] + zrecv[p, s].astype(F32)
 
     erecv[zed] = retst[zed]
 
     def entry_to_neighbour(at):
         return remote(yesend.at[at], yerecv.at[at], yes_, yer(at), ctx=neighbour)
 
-    def mate_copy(i):
-        return remote(e2send.at[i], e2recv.at[i], e2s, e2r, ctx=mate)
+    def mate_copy(i, group):
+        return remote(e2send.at[i], e2recv.at[i], e2s, e2r(group), ctx=mate)
 
     def for_cores(i, s, e):
         down, theirs = decays(s, i)
@@ -502,7 +502,7 @@
         entry_to_neighbour(at).start()
         for s in range(prompts):
             for_cores(i, s, entries[s])
-        mate_copy(i).start()
+        mate_copy(i, 0).start()
 
     entry_step(zed)
 
@@ -665,14 +665,15 @@
             entry_to_neighbour(at).wait_recv()
             for s in range(prompts):
                 for_cores(i, s, yerecv[at, s].astype(F32))
-            mate_copy(i).start()
+            mate_copy(i, 1).start()
             finish_mine(i)
 
-    def other_core():
-        wait_got(e2r, e2recv)
-
-        @pl.loop(0, CHIPS)
-        def _(i):
+    def other_core(group, column):
+        wait_got(e2r(group), e2recv.at[:PAIRS])
+
+        @pl.loop(0, PAIRS)
+        def _(k):
+            i = 2 * k + column
             for s in range(prompts):
                 finish(s, (1 - core) * CHIPS + i, e2recv[i, s])
 
@@ -718,6 +719,8 @@
 
         if h == 0:
             own_column()
+        if h == 1:
+            other_core(0, why)
         wait_got(gfr(h), gbuf.at[0])
         wait_got(qr(h), ssqr.at[h, : CTX - 1])
 
@@ -738,7 +741,7 @@
         if h == FINISH[0]:
             other_column()
         if h == FINISH[1]:
-            other_core()
+            other_core(1, 1 - why)
 
     rbuf[t] = fstage[:, rows_of(t), :]
 
@@ -864,8 +867,8 @@
         V(pairs, BF16),
         V(pairs, BF16),
         V(pairs, F32),
-        V(pairs, F32),
-        V(pairs, F32),
+        V(pairs, BF16),
+        V(pairs, BF16),
         V((prompts, states, LANES), F32),
         V(pairs, BF16),
         V(pairs, BF16),
@@ -885,7 +888,7 @@
         V((steps, rows, out_width), BF16),
         V((TP, steps, rows // TP, out_width), BF16),
         dma((8,)),
-        dma((86,)),
+        dma((87,)),
     ]
     prefill, layer = pl.pallas_call(
         kernel,

time: 67.9 us -> 62 us (0.913)
  Pallas kernels: 67.1 us -> 60.6 us
    pallas_call x1, Pallas kernels: 65 us -> 58.5 us  [shards(): pl.pallas_call(kernel, out_shape=(jax.ShapeDtypeStruct((prompts, tokens,...]
where the time goes in v3:
time: 62 us; the launch traced here: 61.2 us
  Pallas kernels  60.6 us (98%)
  between operations  0.65 us (1%)
    pallas_call x1, Pallas kernels, shards(): pl.pallas_call(kernel, out_shape=(jax.ShapeDtypeStruct((prompts, tokens,...  58.5 us
    pallas_call x1, Pallas kernels, shards(): pl.pallas_call(hand_on, out_shape=tuple((jax.ShapeDtypeStruct(shape, BF16...  2.04 us

profile of v3, /device:TPU:1, one launch (start us, length us, event | category | flops | bytes accessed | tf_op | source)
XLA Modules:
  0.0 61.2 jit_solution(1583430757199759215)
XLA Ops:
  0.6 58.5 %mixer.1 = (bf16[2,128,2048]{2,1,0:T(8,128)(2,1)}, bf16[4,16,512]{2,1,0:T(8,128)(2,1)}) custom-call(bf16[2,128,2048]{2,1,0:T(8,128)(2,1)} %x_hbm.1, bf16[2,128,512]{2,1,0:T(8,128)(2,1)} %bitcast.16, bf16[2,128,2048]{2,1,0:T(8,128)(2,1)} %z_hbm.1, f32[2,32,128]{2,1,0:T(8,128)} %dt_ref.1, f32[1,32]{1,0:T(1,128)} %bitcast.23, f32[1,32]{1,0:T(1,128)} %bitcast.24, ...), custom_call_target="tpu_custom_call" | custom-call | tf_op jit(solution)/shard_map/mixer/pallas_call | solution.py:893
  59.2 2.0 %results.1 = (bf16[2,128,2048]{2,1,0:T(8,128)(2,1)}, bf16[4,16,512]{2,1,0:T(8,128)(2,1)}) custom-call(bf16[2,128,2048]{2,1,0:T(8,128)(2,1)} %get-tuple-element.4.a_hbm, bf16[4,16,512]{2,1,0:T(8,128)(2,1)} %get-tuple-element.5.b_hbm), custom_call_target="tpu_custom_call" | custom-call | tf_op jit(solution)/shard_map/results/pallas_call | solution.py:916
